TPU v7x, 512 devices: a 4x2x32 block of a 4x16x32 slice. The times are simulated.
512 devices in a mesh: groups: 2 (over y), word: 32 (over z), sub: 8 (over x, core).
Axes of the slice: x: 4, y: 2, z: 32, core: 2. Of those that a mesh axis runs over, the one named last changes fastest.
The devices are a block of a 4x16x32 slice.
Arguments:
- word_ids: int32 [32, 32, 4096], P('word', None, 'groups'), parts along dimension 2, may hold values from 0 to 32767
- word_weights: float32 [32, 32, 4096], P('word', None, 'groups'), parts along dimension 2, may hold values from 0.25 to 12
- neighbours: int32 [50, 4096], P(None, 'groups'), parts along dimension 1, may hold values from 0 to 2047
- descriptors: bfloat16 [4096, 128, 128], P(('groups', 'word'), 'sub'), parts along dimension 0, may hold values from -6 to 6
- keypoint_count: int32 [4096], P('groups'), parts along dimension 0, may hold values from 32 to 128
- send_table: int32 [64, 32, 8, 2], P('groups'), parts along dimension 0, may hold values from 0 to 63
- pair_slots: int32 [64, 8, 32, 2], P(('groups', 'word'), 'sub'), parts along dimension 0, may hold values from 0 to 63, as said below
Outputs:
- similarity: float32 [4096, 50], P(('groups', 'word', 'sub')), parts along dimension 0
- nearest: float32 [64, 8, 32, 128], P(('groups', 'word'), 'sub'), parts along dimension 0
- margin: float32 [64, 8, 32, 128], P(('groups', 'word'), 'sub'), parts along dimension 0
There are 2 independent parts, one for each index of `groups`. A program takes and returns all parts, laid end to end along the dimension named above; each array names one. Nothing has to cross between parts.
Inputs may be any that keep to these rules, and one draw needn't show every extreme that they name: `word_ids`: each image has 32 word occurrences in every vocabulary shard, given as word numbers within that shard; a number may repeat. `keypoint_count`: keypoint slots at and beyond an image's count are padding. send_table[v, w, s, c] is an image counted among word index v's 64 stored images; every device receives exactly 2 images from every word index, and one image may go to many devices. `pair_slots`: the two slots of a pair are different slots among the 64 of that device, the query first.
All inputs are finite; a program needn't handle non-finite values.
Results may differ from a plain program's by a relative error of at most 0.0003.
Values may be sent and summed in bfloat16 or wider, within the bound.
No kernel may reach another device: no remote copies, remote signals or barrier semaphores. Data moves between devices by JAX's collectives and lax.ppermute only.
A program may use at most 64 MiB of HBM per device.

v0:
```python
import functools

import jax
import jax.numpy as jnp
from jax import lax
from jax.experimental import pallas as pl
from jax.experimental.pallas import tpu as pltpu
from jax.sharding import PartitionSpec as P


INTERPRET = False
F32, BF16, I32 = jnp.float32, jnp.bfloat16, jnp.int32
LANES = 128
PENALTY = 1e30
SMEM = pltpu.SMEM
VMEM = pltpu.VMEM
GROUPS = (8,)


def call(body, outs, ins, specs=None, scratch=(), mebibytes=2):
    specs = specs or [vm() for _ in ins]
    single = not isinstance(outs, (list, tuple))
    out_list = [outs] if single else list(outs)
    ins = [
        pltpu.with_memory_space_constraint(x, VMEM) if spec.memory_space is VMEM and not INTERPRET else x
        for x, spec in zip(ins, specs)
    ]
    gridded = any(spec.block_shape is not None for spec in specs)
    result = pl.pallas_call(
        body,
        out_shape=[x if INTERPRET else VMEM(x.shape, x.dtype) for x in out_list],
        in_specs=specs,
        out_specs=[vm() for _ in out_list],
        **({"grid": (1,)} if gridded else {}),
        scratch_shapes=list(scratch),
        compiler_params=pltpu.CompilerParams(vmem_limit_bytes=mebibytes << 20),
        interpret=INTERPRET,
    )(*ins)
    return result[0] if single else result


def vm():
    return pl.BlockSpec(memory_space=VMEM)


def sm():
    return pl.BlockSpec(memory_space=SMEM)


def struct(shape, dtype=BF16):
    return jax.ShapeDtypeStruct(shape, dtype)


def rounded(x):
    return x.astype(BF16).astype(F32)


def split3(x):
    first = rounded(x)
    rest = x - first
    second = rounded(rest)
    return first, second, rounded(rest - second)


def encode(norms, dots):
    high = rounded(norms)
    low = rounded(norms - high)
    return jnp.concatenate((high, low) + split3(dots), axis=0).astype(BF16)


def decode(tile):
    wide = tile.astype(F32)
    norms = wide[0:2] + wide[2:4]
    dots = (wide[4:8] + wide[8:12]) + wide[12:16]
    return norms, dots, wide[0:4]


def re_encode(head, dots):
    return jnp.concatenate((head,) + split3(dots), axis=0).astype(BF16)


def spread(rows):
    turned = pltpu.roll(rows, 64, 1)
    low = lax.broadcasted_iota(I32, rows.shape, 1) < 64
    return jnp.where(low, rows, turned), jnp.where(low, turned, rows)


def staggered(four):
    group = lax.broadcasted_iota(I32, four.shape, 1) // 32
    out = four
    for g in range(1, 4):
        out = jnp.where(group == g, pltpu.roll(four, LANES - 8 * g, 1), out)
    return out


def lane_sums(products):
    ones = jnp.ones((8, LANES), F32)
    return lax.dot_general(
        ones, products, (((1,), (1,)), ((), ())), precision=lax.Precision.HIGHEST, preferred_element_type=F32
    )


def norm_kernel(ids_ref, values_ref, out_ref):
    for j in range(out_ref.shape[0]):
        lanes = slice(j * LANES, (j + 1) * LANES)
        ids, values = ids_ref[:, lanes], values_ref[:, lanes]
        acc = jnp.zeros_like(values)
        for b in range(ids_ref.shape[0]):
            acc = acc + jnp.where(ids == ids_ref[b : b + 1, lanes], values_ref[b : b + 1, lanes], 0.0)
        out_ref[j : j + 1, :] = jnp.sum(acc * values, axis=0, keepdims=True)


def cross_kernel(count, table_ref, rows_f, rows_b, idx_f, idx_b, dep_ref, out_ref, turned, gathered, products):
    del dep_ref
    padded = gathered.shape[0]
    images = rows_f.shape[1]
    gathered[...] = jnp.zeros_like(gathered)
    products[...] = jnp.zeros_like(products)
    for which, (rows_ref, idx_ref) in enumerate(((rows_f, idx_f), (rows_b, idx_b))):
        ids, weights = spread(rows_ref[0])
        other, value = staggered(ids), staggered(weights)
        for t in range(8):
            turned[0, t] = pltpu.roll(other, LANES - t, 1) if t else other
            turned[1, t] = pltpu.roll(value, LANES - t, 1) if t else value

        def image(i, carry):
            for k in range(count):
                row = idx_ref[0, 0, i * count + k]
                gathered[k : k + 1, :] = table_ref[row]
            queries = [turned[0, t, pl.ds(i, 1), :] for t in range(8)]
            scales = [turned[1, t, pl.ds(i, 1), :] for t in range(8)]
            for part in range(padded // 8):
                near_ids, near_weights = spread(gathered[part * 8 : part * 8 + 8, :])
                acc = jnp.zeros_like(near_ids)
                for t in range(8):
                    acc = acc + jnp.where(near_ids == queries[t], scales[t], 0.0)
                start = pl.multiple_of(i * padded + part * 8, 8)
                products[pl.ds(start, 8), :] = acc * near_weights
            return carry

        lax.fori_loop(0, images, image, 0)
        sums = lane_sums(products[...])
        for j in range(4):
            out_ref[which, j : j + 1, :] = sums[0:1, j * LANES : (j + 1) * LANES]


def first_kernel(desc_ref, norm_ref, cross_ref, out):
    held = desc_ref.shape[0]
    out[0:held] = desc_ref[...]
    for e in range(2):
        out[held + e] = encode(norm_ref[2 * e : 2 * e + 2], cross_ref[e])


def merge_kernel(skip, recv, norm_ref, cross_ref, out, norm_out):
    kept = out.shape[0] - 2
    last = recv.shape[0] - 2
    out[0:kept] = recv[skip : skip + kept]
    for e in range(2):
        norms, dots, head = decode(recv[last + e])
        out[kept + e] = re_encode(head, dots + cross_ref[e])
        norm_out[2 * e : 2 * e + 2] = norm_ref[2 * e : 2 * e + 2] + norms


def trim_kernel(idx, recv_a, recv_b, norm_ref, cross_ref, out_a, out_b, norm_out):
    kept = out_a.shape[0]
    last = recv_b.shape[0] - 2
    for n in range(kept):
        out_a[n] = recv_a[idx[n]]
        out_b[n] = recv_b[idx[n]]
    for e in range(2):
        norms, dots, head = decode(recv_b[last + e])
        out_b[kept + e] = re_encode(head, dots + cross_ref[e])
        norm_out[2 * e : 2 * e + 2] = norm_ref[2 * e : 2 * e + 2] + norms


def select_kernel(subs, distances, info, idx, *refs):
    out = refs[-1]
    core = info[0]
    at = 0
    step = 0
    for d in distances:
        row = 2 * d - 1 + core if d else 0
        for s in range(subs):
            for c in range(2):
                slot = idx[row * 2 * subs + s * 2 + c]
                if d:
                    out[s, 4 * step + 2 * c + core] = refs[at][slot]
                    out[s, 4 * step + 2 * c + 1 - core] = refs[at + 1][slot]
                else:
                    out[s, 4 * (len(distances) - 1) + c] = refs[at][slot]
        at += 2 if d else 1
        step += 1 if d else 0


def tail_kernel(subs, info, *refs):
    blocks, (norm_ref, kept_ref, out) = refs[:-3], refs[-3:]
    core = info[0]
    last = len(blocks) // 2 - 1
    for j in range(last + 1):
        for q, src in ((core, blocks[2 * j]), (1 - core, blocks[2 * j + 1])):
            for s in range(subs):
                for c in range(2):
                    slot = 2 * s + c if j < last else 2 * (s % (subs // 2)) + c
                    out[s, 4 * j + 2 * c + q] = src[slot]
    recv = blocks[-1]
    size = recv.shape[0] - 2
    upward = core == 0
    totals = []
    empty = jnp.zeros((4, LANES), F32)
    for e in range(2):
        norms, dots, _ = decode(recv[size + e])
        totals.append(norm_ref[2 * e : 2 * e + 2] + jnp.where(upward, norms, 0.0))
        own = jnp.where(upward, dots, kept_ref[e])
        tile = jnp.concatenate(split3(own) + (empty,), axis=0).astype(BF16)
        for s in range(subs // 2):
            out[2 * s + e, 4 * last + 5] = tile
    tile = jnp.concatenate(split3(jnp.concatenate(totals, axis=0)) + (empty,), axis=0).astype(BF16)
    for s in range(subs):
        out[s, 4 * last + 4] = tile


def keep_kernel(recv, cross_ref, out):
    last = recv.shape[0] - 2
    for e in range(2):
        _, dots, _ = decode(recv[last + e])
        out[e] = dots + cross_ref[e]


def joined(tile):
    wide = tile.astype(F32)
    return (wide[0:4] + wide[4:8]) + wide[8:12]


def match_kernel(count, plan, width, topk, padded, pairs, info, *refs):
    groups = refs[:count]
    pen, live, near_row, near_lane, own_row, own_lane = refs[count : count + 6]
    nearest, margin, similarity = refs[count + 6 : count + 9]
    lhs, rhs, squares, least, less, query = refs[count + 9 :]
    pair_total = nearest.shape[0]
    subs = groups[0].shape[0]
    depth = groups[0].shape[2]
    wide = subs * depth
    end = groups[-1].shape[1]

    near = jnp.zeros(near_row.shape, F32)
    own = jnp.zeros(near_row.shape, F32)
    for x in range(subs // 2):
        rows = joined(groups[-1][2 * x, end - 2]) + joined(groups[-1][2 * x + 1, end - 2])
        for h in range(4):
            line = jnp.broadcast_to(rows[h : h + 1], near_row.shape)
            at = jnp.take_along_axis(line, near_lane[...], axis=1)
            near = jnp.where(near_row[...] == 4 * x + h, at, near)
            at = jnp.take_along_axis(line, own_lane[...], axis=1)
            own = jnp.where(own_row[...] == 4 * x + h, at, own)
    chip = info[1]
    dots = joined(groups[-1][2 * chip, end - 1]) + joined(groups[-1][2 * chip + 1, end - 1])
    cosine = dots / jnp.sqrt(own * near)
    for r in range(similarity.shape[0]):
        line, lane = divmod(r * padded, LANES)
        both = jnp.concatenate((cosine[line : line + 1], cosine[line + 1 : line + 2]), axis=1) if line < 3 else cosine[3:4]
        similarity[r : r + 1, :] = both[:, lane : lane + topk]

    tail = rhs.shape[1] - wide
    row = lax.broadcasted_iota(I32, (tail, LANES), 0)
    ones = jnp.where(row < 4, 1.0, 0.0).astype(BF16)

    def prepare(slot, blocks):
        total = jnp.zeros((depth, LANES), F32)
        for s, block in enumerate(blocks):
            rhs[slot, s * depth : (s + 1) * depth, :] = block
            value = block.astype(F32)
            lhs[slot, s * depth : (s + 1) * depth, :] = (value * -2.0).astype(BF16)
            total = total + value * value
        square = jnp.sum(total, axis=0, keepdims=True)
        squares[pl.ds(slot, 1), :] = square
        parts = split3(square)
        extra = jnp.where(row == 0, parts[0], 0.0)
        extra = jnp.where(row == 1, parts[1], extra)
        extra = jnp.where(row == 2, parts[2], extra)
        extra = jnp.where(row == 3, pen[pl.ds(slot, 1), :], extra)
        lhs[slot, wide:, :] = extra.astype(BF16)
        rhs[slot, wide:, :] = ones

    for which, first, positions, ways, at in plan:
        group = groups[which]

        def image(i, carry, group=group, first=first, ways=ways, at=at):
            if ways == 0:
                prepare(i, [group[s, at + i] for s in range(subs)])
                return carry
            source = i // 2
            step = source // ways
            lineage = source - ways * step if ways == 2 else info[2]
            tile = at + 4 * step + 2 * (i - 2 * source)
            prepare(2 * first + i, [group[2 * (s // 2) + lineage, tile + s % 2] for s in range(subs)])
            return carry

        lax.fori_loop(0, 2 * positions, image, 0)

    def pair(p, carry):
        asked = pairs[2 * p]
        refer = pairs[2 * p + 1]
        scores = lax.dot_general(
            lhs[refer], rhs[asked], (((0,), (0,)), ((), ())), preferred_element_type=F32
        )
        first = scores[0:8]
        second = jnp.full_like(first, PENALTY)
        for b in range(1, LANES // 8):
            value = scores[8 * b : 8 * b + 8]
            second = jnp.minimum(second, jnp.maximum(first, value))
            first = jnp.minimum(first, value)
        least[p] = first
        less[p] = second
        query[pl.ds(p, 1), :] = squares[pl.ds(asked, 1), :]
        return carry

    lax.fori_loop(0, pair_total, pair, 0)
    first = least[:, 0, :]
    second = less[:, 0, :]
    for b in range(1, 8):
        other, runner = least[:, b, :], less[:, b, :]
        second = jnp.minimum(jnp.maximum(first, other), jnp.minimum(second, runner))
        first = jnp.minimum(first, other)
    alive = live[...] > 0.0
    nearest[...] = jnp.where(alive, (first + query[...]) * (1.0 / width), 0.0)
    margin[...] = jnp.where(alive, (second - first) * (1.0 / width), 0.0)


def local(word_ids, word_weights, neighbours, descriptors, keypoint_count, send_table, pair_slots):
    words = lax.axis_size("word")
    subs = lax.axis_size("sub")
    w = lax.axis_index("word")
    s = lax.axis_index("sub")
    core = lax.rem(s, 2)
    reach = words // 2
    pairs_of_ring = [
        (i * subs + j, ((i + (1 if j % 2 == 0 else words - 1)) % words) * subs + j)
        for i in range(words)
        for j in range(subs)
    ]
    _, images = word_ids.shape[1:]
    topk = neighbours.shape[0]
    padded = -(-topk // 8) * 8
    per = images // (words * subs)
    held, depth, points = descriptors.shape
    targets = 2 * subs
    width = depth * subs
    pair_total = pair_slots.shape[2]

    def send(x):
        return lax.ppermute(x, ("word", "sub"), pairs_of_ring)

    a = send(descriptors)
    partner = lax.ppermute(descriptors, "sub", [(j, j ^ 1) for j in range(subs)])

    wide_ids = word_ids[0].astype(F32)
    ids = jnp.transpose(wide_ids, (1, 0))
    values = jnp.transpose(word_weights[0], (1, 0))
    table = jnp.concatenate((ids, ids, values, values), axis=1)
    chips = subs // 2
    chip = s // 2
    mine = lax.dynamic_index_in_dim(table.reshape(words, chips, 2 * per, LANES), chip, 1, keepdims=False)
    near = lax.dynamic_index_in_dim(neighbours.reshape(topk, words, chips, 2 * per), chip, 2, keepdims=False)
    near = jnp.transpose(near, (1, 2, 0)).reshape(words, 2 * per * topk)
    count = jnp.arange(1, reach + 1, dtype=I32)
    turn = lax.rem(w + jnp.where(core == 0, reach + 1 - count, reach + count), words)
    mine_order = mine[turn].reshape(2 * reach, per, LANES)
    near_order = near[turn].reshape(2 * reach, 1, per * topk)
    table3 = table.reshape(images, 1, LANES)
    share = images // chips
    norm = call(
        norm_kernel,
        struct((share // LANES, LANES), F32),
        (
            lax.dynamic_slice_in_dim(wide_ids, chip * share, share, 1),
            lax.dynamic_slice_in_dim(word_weights[0], chip * share, share, 1),
        ),
    )

    def cross(k, dep):
        block = lambda e: pl.BlockSpec((1, per, LANES), lambda i: (2 * k - 2 + e, 0, 0))
        index = lambda e: pl.BlockSpec((1, 1, per * topk), lambda i: (2 * k - 2 + e, 0, 0), memory_space=SMEM)
        return call(
            functools.partial(cross_kernel, topk),
            struct((2, 4, LANES), F32),
            (table3, mine_order, mine_order, near_order, near_order, dep),
            [vm(), block(0), block(1), index(0), index(1), vm()],
            (
                pltpu.VMEM((2, 8, 8, LANES), F32),
                pltpu.VMEM((padded, LANES), F32),
                pltpu.VMEM((4 * LANES, LANES), F32),
            ),
        )

    order = [0]
    for d in range(1, reach):
        order += [words - d, d]
    order += [reach]
    source = lax.rem(w + jnp.array(order, I32), words)
    taken = lax.dynamic_index_in_dim(send_table, w, 1, keepdims=False).reshape(words, targets)[source]
    flat_taken = taken.reshape(-1)
    own_images = lax.dynamic_slice_in_dim(taken, 2 * s, 2, 1) + source[:, None] * held
    own_count = keypoint_count[own_images.reshape(-1)]
    column = jnp.arange(points, dtype=I32)[None, :]
    pen = jnp.where(column < own_count[:, None], 0.0, PENALTY).astype(F32)
    pairs = pair_slots[0, 0]
    delta = lax.rem(pairs // 2 - w + words, words)
    place = jnp.where(delta < reach, 2 * delta, 2 * (words - delta) - 1)
    pairs = place * 2 + lax.rem(pairs, 2)
    live = jnp.where(column < own_count[pairs[:, 0]][:, None], 1.0, 0.0).astype(F32)
    flat_pairs = pairs.reshape(-1)
    sign = 1 - 2 * core
    ahead = lax.rem(w + sign * jnp.arange(1, 5, dtype=I32) + words, words)
    behind = lax.rem(w - sign * (reach - 4) + words, words)
    trims = lax.dynamic_index_in_dim(send_table, behind, 0, keepdims=False).reshape(words, targets)[ahead]
    trims = jnp.concatenate((trims[:3].reshape(-1), lax.dynamic_slice_in_dim(trims[3], core * subs, subs, 0)))
    info = jnp.stack((core, chip, s // chips, core)).astype(I32)

    at_own = (w * subs + s) * per
    listed = jnp.transpose(lax.dynamic_slice_in_dim(neighbours, at_own, per, 1), (1, 0))
    listed = jnp.pad(listed, ((0, 0), (0, padded - topk)))
    itself = at_own + jnp.arange(per, dtype=I32)[:, None] + jnp.zeros((1, padded), I32)

    def locate(image):
        flat = jnp.pad(image.reshape(-1), (0, 4 * LANES - per * padded)).reshape(4, LANES)
        return flat // LANES, lax.rem(flat, LANES)

    near_row, near_lane = locate(listed)
    own_row, own_lane = locate(itself)

    def select(distances, blocks):
        refs = [block for pair in blocks for block in pair]
        own = 2 if distances[0] == 0 else 0
        chosen = call(
            functools.partial(select_kernel, subs, distances),
            struct((subs, 4 * (len(distances) - own // 2) + own, depth, points)),
            (info, flat_taken, *refs),
            [sm(), sm()] + [vm()] * len(refs),
        )
        return lax.all_to_all(chosen, "sub", 0, 0, tiled=True)

    norm_struct = struct((share // LANES, LANES), F32)
    first = (partner, norm, cross(1, descriptors))
    b = send(call(first_kernel, struct((held + 2, depth, points)), first))
    norm = jnp.where(core == 0, norm, 0.0)
    blocks = [(descriptors,), (a, b)]
    exchange = []
    plan = []
    start = 0
    full = reach - 4

    def deliver(stop):
        plan.append((len(exchange), max(2 * start - 1, 1), 2 * (stop - max(start, 1) + 1), 2, 0))
        if start == 0:
            plan.append((0, 0, 1, 0, 4 * stop))
        exchange.append(select(list(range(start, stop + 1)), blocks[start : stop + 1]))

    for k in range(2, full + 1):
        product = cross(k, a)
        a = send(a)
        merged, norm = call(
            functools.partial(merge_kernel, 0), (struct((held + 2, depth, points)), norm_struct), (b, norm, product)
        )
        b = send(merged)
        if k - 1 in GROUPS:
            deliver(k - 1)
            start = k
        blocks.append((a, b))
    size = 3 * targets + subs
    a, b, norm = call(
        trim_kernel,
        (struct((size, depth, points)), struct((size + 2, depth, points)), norm_struct),
        (trims, a, b, norm, cross(full + 1, a)),
        [sm()] + [vm()] * 4,
    )
    a, b = send(a), send(b)
    deliver(full)
    last = [a, b]
    for k in range(full + 2, reach + 1):
        size -= targets
        product = cross(k, a)
        if k == reach:
            kept = call(keep_kernel, struct((2, 4, LANES), F32), (b, product))
        a = send(a[targets:])
        merged, norm = call(
            functools.partial(merge_kernel, targets),
            (struct((size + 2, depth, points)), norm_struct),
            (b, norm, product),
        )
        b = send(merged)
        last += [a, b]
    steps = len(last) // 2
    tail = call(
        functools.partial(tail_kernel, subs),
        struct((subs, 4 * steps + 2, depth, points)),
        (info, *last, norm, kept),
        [sm()] + [vm()] * (len(last) + 2),
    )
    plan.append((len(exchange), 2 * full + 1, 2 * (steps - 1), 2, 0))
    plan.append((len(exchange), 2 * reach - 1, 1, 1, 4 * (steps - 1)))
    exchange.append(lax.all_to_all(tail, "sub", 0, 0, tiled=True))

    total = 2 * words
    ins = (flat_pairs, info, *exchange, pen, live, near_row, near_lane, own_row, own_lane)
    rows = struct((pair_total, points), F32)
    nearest, margin, similarity = call(
        functools.partial(match_kernel, len(exchange), plan, width, topk, padded),
        (rows, rows, struct((per, topk), F32)),
        ins,
        [sm(), sm()] + [vm()] * (len(ins) - 2),
        (
            pltpu.VMEM((total, width + depth, points), BF16),
            pltpu.VMEM((total, width + depth, points), BF16),
            pltpu.VMEM((total, points), F32),
            pltpu.VMEM((pair_total, 8, points), F32),
            pltpu.VMEM((pair_total, 8, points), F32),
            pltpu.VMEM((pair_total, points), F32),
        ),
        8,
    )
    return similarity, nearest[None, None], margin[None, None]


def solution(mesh):
    in_specs = (
        P("word", None, "groups"),
        P("word", None, "groups"),
        P(None, "groups"),
        P(("groups", "word"), "sub", None),
        P("groups"),
        P("groups", None, None, None),
        P(("groups", "word"), "sub", None, None),
    )
    out_specs = (
        P(("groups", "word", "sub"), None),
        P(("groups", "word"), "sub", None, None),
        P(("groups", "word"), "sub", None, None),
    )

    return jax.shard_map(local, mesh=mesh, in_specs=in_specs, out_specs=out_specs, check_vma=False)
```

profile of v0, /device:TPU:38, one launch (start us, length us, event | category | flops | bytes accessed | tf_op | source)
XLA Modules:
  0.0 332.4 jit_solution(3062086613490664272)
XLA Ops:
  19.6 4.7 %collective-permute-start.2 = (bf16[66,16,128]{2,1,0:T(8,128)(2,1)S(1)}, bf16[66,16,128]{2,1,0:T(8,128)(2,1)S(1)}, u32[]{:S(2)}, u32[]{:S(2)}) collective-permute-start(bf16[66,16,128]{2,1,0:T(8,128)(2,1)S(1)} %shard_map.105), channel_id=1, source_target_pairs={{0,8},{1,249},{2,10},{3,251},{4,12},{5,253},{6,14},{7,255},{8,16},... | collective-permute-start | bytes 811016 | tf_op jit(solution)/shard_map/ppermute | solution.py:351
  24.3 4.7 %collective-permute-start = (bf16[64,16,128]{2,1,0:T(8,128)(2,1)S(1)}, bf16[64,16,128]{2,1,0:T(8,128)(2,1)S(1)}, u32[]{:S(2)}, u32[]{:S(2)}) collective-permute-start(bf16[64,16,128]{2,1,0:T(8,128)(2,1)S(1)} %copy-done.18), channel_id=1, source_target_pairs={{0,8},{1,249},{2,10},{3,251},{4,12},{5,253},{6,14},{7,255},{8,16},... | collective-permute-start | bytes 786440 | tf_op jit(solution)/shard_map/ppermute | solution.py:351
  29.0 43.1 %collective-permute-done.dep_ref.refs_1_ = bf16[64,16,128]{2,1,0:T(8,128)(2,1)S(1)} collective-permute-done((bf16[64,16,128]{2,1,0:T(8,128)(2,1)S(1)}, bf16[64,16,128]{2,1,0:T(8,128)(2,1)S(1)}, u32[]{:S(2)}, u32[]{:S(2)}) %collective-permute-start) | collective-permute-done | bytes 262176 | tf_op jit(solution)/shard_map/ppermute | solution.py:351
  79.7 8.5 %collective-permute-done.3.dep_ref.refs_3_ = bf16[64,16,128]{2,1,0:T(8,128)(2,1)S(1)} collective-permute-done((bf16[64,16,128]{2,1,0:T(8,128)(2,1)S(1)}, bf16[64,16,128]{2,1,0:T(8,128)(2,1)S(1)}, u32[]{:S(2)}, u32[]{:S(2)}) %collective-permute-start.3) | collective-permute-done | bytes 262176 | tf_op jit(solution)/shard_map/ppermute | solution.py:351
  95.7 8.5 %collective-permute-done.5.dep_ref.refs_5_ = bf16[64,16,128]{2,1,0:T(8,128)(2,1)S(1)} collective-permute-done((bf16[64,16,128]{2,1,0:T(8,128)(2,1)S(1)}, bf16[64,16,128]{2,1,0:T(8,128)(2,1)S(1)}, u32[]{:S(2)}, u32[]{:S(2)}) %collective-permute-start.5) | collective-permute-done | bytes 262176 | tf_op jit(solution)/shard_map/ppermute | solution.py:351
  111.7 8.5 %collective-permute-done.7.dep_ref.refs_7_ = bf16[64,16,128]{2,1,0:T(8,128)(2,1)S(1)} collective-permute-done((bf16[64,16,128]{2,1,0:T(8,128)(2,1)S(1)}, bf16[64,16,128]{2,1,0:T(8,128)(2,1)S(1)}, u32[]{:S(2)}, u32[]{:S(2)}) %collective-permute-start.7) | collective-permute-done | bytes 262176 | tf_op jit(solution)/shard_map/ppermute | solution.py:351
  127.7 8.5 %collective-permute-done.9.dep_ref.refs_9_ = bf16[64,16,128]{2,1,0:T(8,128)(2,1)S(1)} collective-permute-done((bf16[64,16,128]{2,1,0:T(8,128)(2,1)S(1)}, bf16[64,16,128]{2,1,0:T(8,128)(2,1)S(1)}, u32[]{:S(2)}, u32[]{:S(2)}) %collective-permute-start.9) | collective-permute-done | bytes 262176 | tf_op jit(solution)/shard_map/ppermute | solution.py:351
  144.4 8.8 %collective-permute-done.11.dep_ref.refs_11_ = bf16[64,16,128]{2,1,0:T(8,128)(2,1)} collective-permute-done((bf16[64,16,128]{2,1,0:T(8,128)(2,1)S(1)}, bf16[64,16,128]{2,1,0:T(8,128)(2,1)}, u32[]{:S(2)}, u32[]{:S(2)}) %collective-permute-start.11) | collective-permute-done | bytes 262176 | tf_op jit(solution)/shard_map/ppermute | solution.py:351
  155.1 3.9 %shard_map.116.cross_ref = f32[2,4,128]{2,1,0:T(4,128)S(1)} custom-call(f32[2048,1,128]{2,1,0:T(1,128)S(1)} %bitcast.105, f32[32,8,128]{2,1,0:T(8,128)S(1)} %bitcast.127, f32[32,8,128]{2,1,0:T(8,128)S(1)} %bitcast.128, s32[32,1,400]{2,1,0:T(1,128)S(1)} %reshape.195.idx_f.idx_b, s32[32,1,400]{2,1,0:T(1,128)S(1)} %reshape.195.idx_f.idx_b, ...), custom_call_target="tpu_custom_call" | custom-call | tf_op jit(solution)/shard_map/pallas_call | solution.py:29
  164.9 3.9 %shard_map.118.cross_ref = f32[2,4,128]{2,1,0:T(4,128)S(1)} custom-call(f32[2048,1,128]{2,1,0:T(1,128)S(1)} %bitcast.106, f32[32,8,128]{2,1,0:T(8,128)S(1)} %bitcast.130, f32[32,8,128]{2,1,0:T(8,128)S(1)} %bitcast.129, s32[32,1,400]{2,1,0:T(1,128)S(1)} %reshape.195.idx_f.idx_b, s32[32,1,400]{2,1,0:T(1,128)S(1)} %reshape.195.idx_f.idx_b, ...), custom_call_target="tpu_custom_call" | custom-call | tf_op jit(solution)/shard_map/pallas_call | solution.py:29
  174.6 3.5 %shard_map.121.cross_ref = f32[2,4,128]{2,1,0:T(4,128)S(1)} custom-call(f32[2048,1,128]{2,1,0:T(1,128)S(1)} %bitcast.107, f32[32,8,128]{2,1,0:T(8,128)S(1)} %bitcast.131, f32[32,8,128]{2,1,0:T(8,128)S(1)} %bitcast.132, s32[32,1,400]{2,1,0:T(1,128)S(1)} %reshape.195.idx_f.idx_b, s32[32,1,400]{2,1,0:T(1,128)S(1)} %reshape.195.idx_f.idx_b, ...), custom_call_target="tpu_custom_call" | custom-call | tf_op jit(solution)/shard_map/pallas_call | solution.py:29
  184.2 3.9 %shard_map.123.cross_ref = f32[2,4,128]{2,1,0:T(4,128)S(1)} custom-call(f32[2048,1,128]{2,1,0:T(1,128)S(1)} %bitcast.108, f32[32,8,128]{2,1,0:T(8,128)S(1)} %bitcast.133, f32[32,8,128]{2,1,0:T(8,128)S(1)} %bitcast.134, s32[32,1,400]{2,1,0:T(1,128)S(1)} %reshape.195.idx_f.idx_b, s32[32,1,400]{2,1,0:T(1,128)S(1)} %reshape.195.idx_f.idx_b, ...), custom_call_target="tpu_custom_call" | custom-call | tf_op jit(solution)/shard_map/pallas_call | solution.py:29
  206.1 4.7 %all-to-all-start = ((bf16[8,34,16,128]{3,2,1,0:T(8,128)(2,1)}), bf16[8,34,16,128]{3,2,1,0:T(8,128)(2,1)S(1)}, u32[]{:S(2)}, u32[]{:S(2)}) async-start(bf16[8,34,16,128]{3,2,1,0:T(8,128)(2,1)} %copy-done.1), calls=%async_computation | async-start | bytes 2228224 | tf_op jit(solution)/shard_map/all_to_all | solution.py:440
  213.3 3.9 %shard_map.125.cross_ref = f32[2,4,128]{2,1,0:T(4,128)S(1)} custom-call(f32[2048,1,128]{2,1,0:T(1,128)S(1)} %bitcast.109, f32[32,8,128]{2,1,0:T(8,128)S(1)} %bitcast.135, f32[32,8,128]{2,1,0:T(8,128)S(1)} %bitcast.136, s32[32,1,400]{2,1,0:T(1,128)S(1)} %reshape.195.idx_f.idx_b, s32[32,1,400]{2,1,0:T(1,128)S(1)} %reshape.195.idx_f.idx_b, ...), custom_call_target="tpu_custom_call" | custom-call | tf_op jit(solution)/shard_map/pallas_call | solution.py:29
  230.9 3.5 %shard_map.130.cross_ref = f32[2,4,128]{2,1,0:T(4,128)S(1)} custom-call(f32[2048,1,128]{2,1,0:T(1,128)S(1)} %bitcast.111, f32[32,8,128]{2,1,0:T(8,128)S(1)} %bitcast.139, f32[32,8,128]{2,1,0:T(8,128)S(1)} %bitcast.140, s32[32,1,400]{2,1,0:T(1,128)S(1)} %reshape.195.idx_f.idx_b, s32[32,1,400]{2,1,0:T(1,128)S(1)} %reshape.195.idx_f.idx_b, ...), custom_call_target="tpu_custom_call" | custom-call | tf_op jit(solution)/shard_map/pallas_call | solution.py:29
  234.5 3.9 %collective-permute-done.24.refs_7_.recv_b = bf16[66,16,128]{2,1,0:T(8,128)(2,1)S(1)} collective-permute-done((bf16[66,16,128]{2,1,0:T(8,128)(2,1)}, bf16[66,16,128]{2,1,0:T(8,128)(2,1)S(1)}, u32[]{:S(2)}, u32[]{:S(2)}) %collective-permute-start.24) | collective-permute-done | bytes 270368 | tf_op jit(solution)/shard_map/ppermute | solution.py:351
  250.6 8.7 %all-to-all-start.1 = ((bf16[8,16,16,128]{3,2,1,0:T(8,128)(2,1)}), bf16[8,16,16,128]{3,2,1,0:T(8,128)(2,1)S(1)}, u32[]{:S(2)}, u32[]{:S(2)}) async-start(bf16[8,16,16,128]{3,2,1,0:T(8,128)(2,1)} %shard_map.129), calls=%async_computation.1 | async-start | bytes 1048576 | tf_op jit(solution)/shard_map/all_to_all | solution.py:440
  273.5 3.5 %shard_map.134.cross_ref = f32[2,4,128]{2,1,0:T(4,128)S(1)} custom-call(f32[2048,1,128]{2,1,0:T(1,128)S(1)} %bitcast.113, f32[32,8,128]{2,1,0:T(8,128)S(1)} %bitcast.143, f32[32,8,128]{2,1,0:T(8,128)S(1)} %bitcast.144, s32[32,1,400]{2,1,0:T(1,128)S(1)} %reshape.195.idx_f.idx_b, s32[32,1,400]{2,1,0:T(1,128)S(1)} %reshape.195.idx_f.idx_b, ...), custom_call_target="tpu_custom_call" | custom-call | tf_op jit(solution)/shard_map/pallas_call | solution.py:29
  278.0 4.5 %collective-permute-start.30 = (bf16[26,16,128]{2,1,0:T(8,128)(2,1)S(1)}, bf16[26,16,128]{2,1,0:T(8,128)(2,1)S(1)}, u32[]{:S(2)}, u32[]{:S(2)}) collective-permute-start(bf16[26,16,128]{2,1,0:T(8,128)(2,1)S(1)} %get-tuple-element.64), channel_id=1, source_target_pairs={{0,8},{1,249},{2,10},{3,251},{4,12},{5,253},{6,14},{7,255},{8,16},... | collective-permute-start | bytes 319496 | tf_op jit(solution)/shard_map/ppermute | solution.py:351
  285.9 3.5 %shard_map.136.cross_ref = f32[2,4,128]{2,1,0:T(4,128)S(1)} custom-call(f32[2048,1,128]{2,1,0:T(1,128)S(1)} %bitcast.114, f32[32,8,128]{2,1,0:T(8,128)S(1)} %bitcast.145, f32[32,8,128]{2,1,0:T(8,128)S(1)} %bitcast.146, s32[32,1,400]{2,1,0:T(1,128)S(1)} %reshape.195.idx_f.idx_b, s32[32,1,400]{2,1,0:T(1,128)S(1)} %reshape.195.idx_f.idx_b, ...), custom_call_target="tpu_custom_call" | custom-call | tf_op jit(solution)/shard_map/pallas_call | solution.py:29
  290.1 3.9 %collective-permute-start.32 = (bf16[10,16,128]{2,1,0:T(8,128)(2,1)S(1)}, bf16[10,16,128]{2,1,0:T(8,128)(2,1)S(1)}, u32[]{:S(2)}, u32[]{:S(2)}) collective-permute-start(bf16[10,16,128]{2,1,0:T(8,128)(2,1)S(1)} %get-tuple-element.66), channel_id=1, source_target_pairs={{0,8},{1,249},{2,10},{3,251},{4,12},{5,253},{6,14},{7,255},{8,16},... | collective-permute-start | bytes 122888 | tf_op jit(solution)/shard_map/ppermute | solution.py:351
  303.4 6.9 %all-to-all-start.2 = ((bf16[8,18,16,128]{3,2,1,0:T(8,128)(2,1)}), bf16[8,18,16,128]{3,2,1,0:T(8,128)(2,1)S(1)}, u32[]{:S(2)}, u32[]{:S(2)}) async-start(bf16[8,18,16,128]{3,2,1,0:T(8,128)(2,1)} %shard_map.139), calls=%async_computation.2 | async-start | bytes 1179648 | tf_op jit(solution)/shard_map/all_to_all | solution.py:501
  310.5 8.8 %all-to-all-done.2.refs_2_ = bf16[8,18,16,128]{3,2,1,0:T(8,128)(2,1)S(1)} async-done(((bf16[8,18,16,128]{3,2,1,0:T(8,128)(2,1)}), bf16[8,18,16,128]{3,2,1,0:T(8,128)(2,1)S(1)}, u32[]{:S(2)}, u32[]{:S(2)}) %all-to-all-start.2) | async-done | bytes 589856 | tf_op jit(solution)/shard_map/all_to_all | solution.py:501
  320.3 10.3 %shard_map.140 = (f32[32,128]{1,0:T(8,128)S(1)}, f32[32,128]{1,0:T(8,128)S(1)}, f32[8,50]{1,0:T(8,128)S(1)}) custom-call(s32[64]{0:T(128)S(1)} %fusion.12.pairs, s32[4]{0:T(128)S(1)} %pad_add_fusion.info, bf16[8,34,16,128]{3,2,1,0:T(8,128)(2,1)S(1)} %all-to-all-done.refs_0_, bf16[8,16,16,128]{3,2,1,0:T(8,128)(2,1)S(1)} %copy-done.3, ...), custom_call_target="tpu_custom_call" | custom-call | tf_op jit(solution)/shard_map/pallas_call | solution.py:29
  (239 shorter events, 154.2 us)
Async XLA Ops:
  0.6 18.9 %collective-permute-start.1 = (bf16[64,16,128]{2,1,0:T(8,128)(2,1)}, bf16[64,16,128]{2,1,0:T(8,128)(2,1)S(1)}, u32[]{:S(2)}, u32[]{:S(2)}) collective-permute-start(bf16[64,16,128]{2,1,0:T(8,128)(2,1)} %refs_0_.1), channel_id=1, source_target_pairs={{0,1},{1,0},{2,3},{3,2},{4,5},{5,4},{6,7},{7,6},{8,9},{9,8},{10,11... | collective-permute-start | bytes 786440 | tf_op jit(solution)/shard_map/ppermute | solution.py:354
  19.6 56.1 %collective-permute-start.2 = (bf16[66,16,128]{2,1,0:T(8,128)(2,1)S(1)}, bf16[66,16,128]{2,1,0:T(8,128)(2,1)S(1)}, u32[]{:S(2)}, u32[]{:S(2)}) collective-permute-start(bf16[66,16,128]{2,1,0:T(8,128)(2,1)S(1)} %shard_map.105), channel_id=1, source_target_pairs={{0,8},{1,249},{2,10},{3,251},{4,12},{5,253},{6,14},{7,255},{8,16},... | collective-permute-start | bytes 811016 | tf_op jit(solution)/shard_map/ppermute | solution.py:351
  24.3 47.9 %collective-permute-start = (bf16[64,16,128]{2,1,0:T(8,128)(2,1)S(1)}, bf16[64,16,128]{2,1,0:T(8,128)(2,1)S(1)}, u32[]{:S(2)}, u32[]{:S(2)}) collective-permute-start(bf16[64,16,128]{2,1,0:T(8,128)(2,1)S(1)} %copy-done.18), channel_id=1, source_target_pairs={{0,8},{1,249},{2,10},{3,251},{4,12},{5,253},{6,14},{7,255},{8,16},... | collective-permute-start | bytes 786440 | tf_op jit(solution)/shard_map/ppermute | solution.py:351
  75.7 16.0 %collective-permute-start.4 = (bf16[66,16,128]{2,1,0:T(8,128)(2,1)S(1)}, bf16[66,16,128]{2,1,0:T(8,128)(2,1)S(1)}, u32[]{:S(2)}, u32[]{:S(2)}) collective-permute-start(bf16[66,16,128]{2,1,0:T(8,128)(2,1)S(1)} %get-tuple-element.37), channel_id=1, source_target_pairs={{0,8},{1,249},{2,10},{3,251},{4,12},{5,253},{6,14},{7,255},{8,16},... | collective-permute-start | bytes 811016 | tf_op jit(solution)/shard_map/ppermute | solution.py:351
  77.7 10.4 %collective-permute-start.3 = (bf16[64,16,128]{2,1,0:T(8,128)(2,1)S(1)}, bf16[64,16,128]{2,1,0:T(8,128)(2,1)S(1)}, u32[]{:S(2)}, u32[]{:S(2)}) collective-permute-start(bf16[64,16,128]{2,1,0:T(8,128)(2,1)S(1)} %collective-permute-done.dep_ref.refs_1_), channel_id=1, source_target_pairs={{0,8},{1,249},{2,10},{3,251},{4,12},{5,253},{6,14},{7,255},{8,16},... | collective-permute-start | bytes 786440 | tf_op jit(solution)/shard_map/ppermute | solution.py:351
  91.7 15.9 %collective-permute-start.6 = (bf16[66,16,128]{2,1,0:T(8,128)(2,1)S(1)}, bf16[66,16,128]{2,1,0:T(8,128)(2,1)S(1)}, u32[]{:S(2)}, u32[]{:S(2)}) collective-permute-start(bf16[66,16,128]{2,1,0:T(8,128)(2,1)S(1)} %get-tuple-element.39), channel_id=1, source_target_pairs={{0,8},{1,249},{2,10},{3,251},{4,12},{5,253},{6,14},{7,255},{8,16},... | collective-permute-start | bytes 811016 | tf_op jit(solution)/shard_map/ppermute | solution.py:351
  93.7 10.4 %collective-permute-start.5 = (bf16[64,16,128]{2,1,0:T(8,128)(2,1)S(1)}, bf16[64,16,128]{2,1,0:T(8,128)(2,1)S(1)}, u32[]{:S(2)}, u32[]{:S(2)}) collective-permute-start(bf16[64,16,128]{2,1,0:T(8,128)(2,1)S(1)} %collective-permute-done.3.dep_ref.refs_3_), channel_id=1, source_target_pairs={{0,8},{1,249},{2,10},{3,251},{4,12},{5,253},{6,14},{7,255},{8,16},... | collective-permute-start | bytes 786440 | tf_op jit(solution)/shard_map/ppermute | solution.py:351
  107.7 16.0 %collective-permute-start.8 = (bf16[66,16,128]{2,1,0:T(8,128)(2,1)S(1)}, bf16[66,16,128]{2,1,0:T(8,128)(2,1)S(1)}, u32[]{:S(2)}, u32[]{:S(2)}) collective-permute-start(bf16[66,16,128]{2,1,0:T(8,128)(2,1)S(1)} %get-tuple-element.41), channel_id=1, source_target_pairs={{0,8},{1,249},{2,10},{3,251},{4,12},{5,253},{6,14},{7,255},{8,16},... | collective-permute-start | bytes 811016 | tf_op jit(solution)/shard_map/ppermute | solution.py:351
  109.7 10.4 %collective-permute-start.7 = (bf16[64,16,128]{2,1,0:T(8,128)(2,1)S(1)}, bf16[64,16,128]{2,1,0:T(8,128)(2,1)S(1)}, u32[]{:S(2)}, u32[]{:S(2)}) collective-permute-start(bf16[64,16,128]{2,1,0:T(8,128)(2,1)S(1)} %collective-permute-done.5.dep_ref.refs_5_), channel_id=1, source_target_pairs={{0,8},{1,249},{2,10},{3,251},{4,12},{5,253},{6,14},{7,255},{8,16},... | collective-permute-start | bytes 786440 | tf_op jit(solution)/shard_map/ppermute | solution.py:351
  123.7 16.0 %collective-permute-start.10 = (bf16[66,16,128]{2,1,0:T(8,128)(2,1)S(1)}, bf16[66,16,128]{2,1,0:T(8,128)(2,1)S(1)}, u32[]{:S(2)}, u32[]{:S(2)}) collective-permute-start(bf16[66,16,128]{2,1,0:T(8,128)(2,1)S(1)} %get-tuple-element.43), channel_id=1, source_target_pairs={{0,8},{1,249},{2,10},{3,251},{4,12},{5,253},{6,14},{7,255},{8,16},... | collective-permute-start | bytes 811016 | tf_op jit(solution)/shard_map/ppermute | solution.py:351
  125.7 10.4 %collective-permute-start.9 = (bf16[64,16,128]{2,1,0:T(8,128)(2,1)S(1)}, bf16[64,16,128]{2,1,0:T(8,128)(2,1)S(1)}, u32[]{:S(2)}, u32[]{:S(2)}) collective-permute-start(bf16[64,16,128]{2,1,0:T(8,128)(2,1)S(1)} %collective-permute-done.7.dep_ref.refs_7_), channel_id=1, source_target_pairs={{0,8},{1,249},{2,10},{3,251},{4,12},{5,253},{6,14},{7,255},{8,16},... | collective-permute-start | bytes 786440 | tf_op jit(solution)/shard_map/ppermute | solution.py:351
  140.4 18.6 %collective-permute-start.12 = (bf16[66,16,128]{2,1,0:T(8,128)(2,1)}, bf16[66,16,128]{2,1,0:T(8,128)(2,1)S(1)}, u32[]{:S(2)}, u32[]{:S(2)}) collective-permute-start(bf16[66,16,128]{2,1,0:T(8,128)(2,1)} %get-tuple-element.45), channel_id=1, source_target_pairs={{0,8},{1,249},{2,10},{3,251},{4,12},{5,253},{6,14},{7,255},{8,16},... | collective-permute-start | bytes 811016 | tf_op jit(solution)/shard_map/ppermute | solution.py:351
  142.4 10.8 %collective-permute-start.11 = (bf16[64,16,128]{2,1,0:T(8,128)(2,1)S(1)}, bf16[64,16,128]{2,1,0:T(8,128)(2,1)}, u32[]{:S(2)}, u32[]{:S(2)}) collective-permute-start(bf16[64,16,128]{2,1,0:T(8,128)(2,1)S(1)} %collective-permute-done.9.dep_ref.refs_9_), channel_id=1, source_target_pairs={{0,8},{1,249},{2,10},{3,251},{4,12},{5,253},{6,14},{7,255},{8,16},... | collective-permute-start | bytes 786440 | tf_op jit(solution)/shard_map/ppermute | solution.py:351
  182.3 29.1 %collective-permute-start.19 = (bf16[64,16,128]{2,1,0:T(8,128)(2,1)}, bf16[64,16,128]{2,1,0:T(8,128)(2,1)}, u32[]{:S(2)}, u32[]{:S(2)}) collective-permute-start(bf16[64,16,128]{2,1,0:T(8,128)(2,1)} %collective-permute-done.17.dep_ref.refs_0_), channel_id=1, source_target_pairs={{0,8},{1,249},{2,10},{3,251},{4,12},{5,253},{6,14},{7,255},{8,16},... | collective-permute-start | bytes 786440 | tf_op jit(solution)/shard_map/ppermute | solution.py:351
  191.0 26.3 %collective-permute-start.20 = (bf16[66,16,128]{2,1,0:T(8,128)(2,1)}, bf16[66,16,128]{2,1,0:T(8,128)(2,1)S(1)}, u32[]{:S(2)}, u32[]{:S(2)}) collective-permute-start(bf16[66,16,128]{2,1,0:T(8,128)(2,1)} %get-tuple-element.53), channel_id=1, source_target_pairs={{0,8},{1,249},{2,10},{3,251},{4,12},{5,253},{6,14},{7,255},{8,16},... | collective-permute-start | bytes 811016 | tf_op jit(solution)/shard_map/ppermute | solution.py:351
  206.1 44.5 %all-to-all-start = ((bf16[8,34,16,128]{3,2,1,0:T(8,128)(2,1)}), bf16[8,34,16,128]{3,2,1,0:T(8,128)(2,1)S(1)}, u32[]{:S(2)}, u32[]{:S(2)}) async-start(bf16[8,34,16,128]{3,2,1,0:T(8,128)(2,1)} %copy-done.1), calls=%async_computation | async-start | bytes 2228224 | tf_op jit(solution)/shard_map/all_to_all | solution.py:440
  239.8 19.4 %collective-permute-start.25 = (bf16[56,16,128]{2,1,0:T(8,128)(2,1)}, bf16[56,16,128]{2,1,0:T(8,128)(2,1)S(1)}, u32[]{:S(2)}, u32[]{:S(2)}) collective-permute-start(bf16[56,16,128]{2,1,0:T(8,128)(2,1)} %get-tuple-element.59), channel_id=1, source_target_pairs={{0,8},{1,249},{2,10},{3,251},{4,12},{5,253},{6,14},{7,255},{8,16},... | collective-permute-start | bytes 688136 | tf_op jit(solution)/shard_map/ppermute | solution.py:351
  241.7 23.9 %collective-permute-start.26 = (bf16[58,16,128]{2,1,0:T(8,128)(2,1)}, bf16[58,16,128]{2,1,0:T(8,128)(2,1)}, u32[]{:S(2)}, u32[]{:S(2)}) collective-permute-start(bf16[58,16,128]{2,1,0:T(8,128)(2,1)} %get-tuple-element.60), channel_id=1, source_target_pairs={{0,8},{1,249},{2,10},{3,251},{4,12},{5,253},{6,14},{7,255},{8,16},... | collective-permute-start | bytes 712712 | tf_op jit(solution)/shard_map/ppermute | solution.py:351
  250.6 52.0 %all-to-all-start.1 = ((bf16[8,16,16,128]{3,2,1,0:T(8,128)(2,1)}), bf16[8,16,16,128]{3,2,1,0:T(8,128)(2,1)S(1)}, u32[]{:S(2)}, u32[]{:S(2)}) async-start(bf16[8,16,16,128]{3,2,1,0:T(8,128)(2,1)} %shard_map.129), calls=%async_computation.1 | async-start | bytes 1048576 | tf_op jit(solution)/shard_map/all_to_all | solution.py:440
  259.9 11.5 %collective-permute-start.27 = (bf16[40,16,128]{2,1,0:T(8,128)(2,1)}, bf16[40,16,128]{2,1,0:T(8,128)(2,1)S(1)}, u32[]{:S(2)}, u32[]{:S(2)}) collective-permute-start(bf16[40,16,128]{2,1,0:T(8,128)(2,1)} %slice.36), channel_id=1, source_target_pairs={{0,8},{1,249},{2,10},{3,251},{4,12},{5,253},{6,14},{7,255},{8,16},... | collective-permute-start | bytes 491528 | tf_op jit(solution)/shard_map/ppermute | solution.py:351
  271.4 11.7 %collective-permute-start.29 = (bf16[24,16,128]{2,1,0:T(8,128)(2,1)S(1)}, bf16[24,16,128]{2,1,0:T(8,128)(2,1)S(1)}, u32[]{:S(2)}, u32[]{:S(2)}) collective-permute-start(bf16[24,16,128]{2,1,0:T(8,128)(2,1)S(1)} %slice.37), channel_id=1, source_target_pairs={{0,8},{1,249},{2,10},{3,251},{4,12},{5,253},{6,14},{7,255},{8,16},... | collective-permute-start | bytes 294920 | tf_op jit(solution)/shard_map/ppermute | solution.py:351
  278.0 11.4 %collective-permute-start.30 = (bf16[26,16,128]{2,1,0:T(8,128)(2,1)S(1)}, bf16[26,16,128]{2,1,0:T(8,128)(2,1)S(1)}, u32[]{:S(2)}, u32[]{:S(2)}) collective-permute-start(bf16[26,16,128]{2,1,0:T(8,128)(2,1)S(1)} %get-tuple-element.64), channel_id=1, source_target_pairs={{0,8},{1,249},{2,10},{3,251},{4,12},{5,253},{6,14},{7,255},{8,16},... | collective-permute-start | bytes 319496 | tf_op jit(solution)/shard_map/ppermute | solution.py:351
  283.8 15.5 %collective-permute-start.31 = (bf16[8,16,128]{2,1,0:T(8,128)(2,1)}, bf16[8,16,128]{2,1,0:T(8,128)(2,1)}, u32[]{:S(2)}, u32[]{:S(2)}) collective-permute-start(bf16[8,16,128]{2,1,0:T(8,128)(2,1)} %slice.38), channel_id=1, source_target_pairs={{0,8},{1,249},{2,10},{3,251},{4,12},{5,253},{6,14},{7,255},{8,16},... | collective-permute-start | bytes 98312 | tf_op jit(solution)/shard_map/ppermute | solution.py:351
  303.4 15.8 %all-to-all-start.2 = ((bf16[8,18,16,128]{3,2,1,0:T(8,128)(2,1)}), bf16[8,18,16,128]{3,2,1,0:T(8,128)(2,1)S(1)}, u32[]{:S(2)}, u32[]{:S(2)}) async-start(bf16[8,18,16,128]{3,2,1,0:T(8,128)(2,1)} %shard_map.139), calls=%async_computation.2 | async-start | bytes 1179648 | tf_op jit(solution)/shard_map/all_to_all | solution.py:501
  (57 other events, 547.1 us)
where the time goes:
time: 337 us; the launch traced here: 332 us
  waiting for transfers between devices  105 us (31%)
  starting transfers between devices  95.4 us (28%)
  Pallas kernels  82.1 us (24%)
  local copies, waits for them, and re-layouts  42.7 us (13%)
  other arithmetic  5.81 us (2%)
    ppermute x32, waiting for transfers between devices, send(): return lax.ppermute(x, ('word', 'sub'), pairs_of_ring)  96.3 us
    pallas_call x38, Pallas kernels, call(): pl.pallas_call(body, out_shape=[x if INTERPRET else VMEM(x.shape, x.dtype...  82.1 us
    ppermute x32, starting transfers between devices, send(): return lax.ppermute(x, ('word', 'sub'), pairs_of_ring)  73.1 us
    unnamed x98, local copies, waits for them, and re-layouts  27.3 us
    all_to_all x2, starting transfers between devices, select(): return lax.all_to_all(chosen, 'sub', 0, 0, tiled=True)  13.3 us
    all_to_all x1, waiting for transfers between devices, local(): exchange.append(lax.all_to_all(tail, 'sub', 0, 0, tiled=True))  8.77 us
    all_to_all x1, starting transfers between devices, local(): exchange.append(lax.all_to_all(tail, 'sub', 0, 0, tiled=True))  6.87 us
  transfers between devices with their start and end apart: 36, of which 16 were waited for; matrix products, arithmetic and copies ran while one was open for 8% of the time, Pallas kernels for 21%

commit v1 on v0

v1 whole, which is shorter than its diff:
```python
import functools

import jax
import jax.numpy as jnp
from jax import lax
from jax.experimental import pallas as pl
from jax.experimental.pallas import tpu as pltpu
from jax.sharding import PartitionSpec as P


INTERPRET = False
F32, BF16, I32 = jnp.float32, jnp.bfloat16, jnp.int32
LANES = 128
PENALTY = 1e30
SMEM = pltpu.SMEM
VMEM = pltpu.VMEM
GROUPS = (8,)


def call(body, outs, ins, specs=None, scratch=(), mebibytes=2, aliases=None, outside=()):
    specs = specs or [vm() for _ in ins]
    single = not isinstance(outs, (list, tuple))
    out_list = [outs] if single else list(outs)
    ins = [
        pltpu.with_memory_space_constraint(x, VMEM) if spec.memory_space is VMEM and not INTERPRET else x
        for x, spec in zip(ins, specs)
    ]
    gridded = any(spec.block_shape is not None for spec in specs)
    result = pl.pallas_call(
        body,
        out_shape=[x if INTERPRET or i in outside else VMEM(x.shape, x.dtype) for i, x in enumerate(out_list)],
        in_specs=specs,
        out_specs=[pl.BlockSpec(memory_space=pl.ANY) if i in outside else vm() for i in range(len(out_list))],
        **({"grid": (1,)} if gridded else {}),
        scratch_shapes=list(scratch),
        input_output_aliases=aliases or {},
        compiler_params=pltpu.CompilerParams(vmem_limit_bytes=mebibytes << 20),
        interpret=INTERPRET,
    )(*ins)
    return result[0] if single else result


def vm():
    return pl.BlockSpec(memory_space=VMEM)


def sm():
    return pl.BlockSpec(memory_space=SMEM)


def struct(shape, dtype=BF16):
    return jax.ShapeDtypeStruct(shape, dtype)


def rounded(x):
    return x.astype(BF16).astype(F32)


def split3(x):
    first = rounded(x)
    rest = x - first
    second = rounded(rest)
    return first, second, rounded(rest - second)


def encode(norms, dots):
    high = rounded(norms)
    low = rounded(norms - high)
    return jnp.concatenate((high, low) + split3(dots), axis=0).astype(BF16)


def decode(tile):
    wide = tile.astype(F32)
    norms = wide[0:2] + wide[2:4]
    dots = (wide[4:8] + wide[8:12]) + wide[12:16]
    return norms, dots, wide[0:4]


def re_encode(head, dots):
    return jnp.concatenate((head,) + split3(dots), axis=0).astype(BF16)


def spread(rows):
    turned = pltpu.roll(rows, 64, 1)
    low = lax.broadcasted_iota(I32, rows.shape, 1) < 64
    return jnp.where(low, rows, turned), jnp.where(low, turned, rows)


def staggered(four):
    group = lax.broadcasted_iota(I32, four.shape, 1) // 32
    out = four
    for g in range(1, 4):
        out = jnp.where(group == g, pltpu.roll(four, LANES - 8 * g, 1), out)
    return out


def lane_sums(products):
    ones = jnp.ones((8, LANES), BF16)
    total = None
    for term in split3(products):
        part = lax.dot_general(ones, term.astype(BF16), (((1,), (1,)), ((), ())), preferred_element_type=F32)
        total = part if total is None else total + part
    return total


def table_kernel(info, ids_ref, values_ref, table_ref, norm_ref):
    occurrences, images = ids_ref.shape
    for j in range(images // LANES):
        lanes = slice(j * LANES, (j + 1) * LANES)
        ids, values = ids_ref[:, lanes].astype(F32), values_ref[:, lanes]
        table_ref[lanes, :] = jnp.concatenate((ids, ids, values, values), axis=0).T
    share = norm_ref.shape[0]
    for j in range(share):
        start = pl.multiple_of((info[1] * share + j) * LANES, LANES)
        ids, values = ids_ref[:, pl.ds(start, LANES)], values_ref[:, pl.ds(start, LANES)]
        acc = jnp.zeros_like(values)
        for b in range(occurrences):
            acc = acc + jnp.where(ids == ids[b : b + 1], values[b : b + 1], 0.0)
        norm_ref[j : j + 1, :] = jnp.sum(acc * values, axis=0, keepdims=True)


def cross_kernel(count, k, turn, words, chosen, info, lists, table_ref, rows_ref, *refs):
    idx, arrived, picked, stored = refs[-4:]
    refs = refs[:-4]
    fetch = pltpu.make_async_copy(lists.at[k - 1], idx, arrived)
    fetch.start()
    if chosen is None:
        out_ref, turned, gathered, products = refs
    else:
        distance, step, paired, fresh = chosen
        taken, refs = refs[0], refs[1:]
        blocks, refs = refs[: 1 + paired], refs[1 + paired + (not fresh) :]
        out_ref, group_ref, turned, gathered, products = refs
        core = info[0]
        for s in range(picked.shape[0]):
            for c in range(2):
                slot = taken[distance * 2 * picked.shape[0] + 2 * s + c]
                if paired:
                    picked[s, 2 * c + core] = blocks[0][slot]
                    picked[s, 2 * c + 1 - core] = blocks[1][slot]
                else:
                    picked[s, c] = blocks[0][slot]
        tiles = 2 + 2 * paired
        store = pltpu.make_async_copy(picked.at[:, 0:tiles], group_ref.at[:, step : step + tiles], stored)
        store.start()
    padded = gathered.shape[1]
    total = turned.shape[2]
    half = total // 2
    up, down = turn
    target = lax.rem(info[3] + jnp.where(info[0] == 0, up, down), words)
    start = pl.multiple_of((target * (rows_ref.shape[0] // (words * total)) + info[1]) * total, total)
    ids, weights = spread(rows_ref[pl.ds(start, total), :])
    other, value = staggered(ids), staggered(weights)
    for t in range(8):
        turned[0, t] = pltpu.roll(other, LANES - t, 1) if t else other
        turned[1, t] = pltpu.roll(value, LANES - t, 1) if t else value
    empty = jnp.zeros((8, LANES), F32)
    for e in range(2):
        gathered[e, padded - 8 :, :] = empty
        for part in range(half * padded // 8, 4 * LANES // 8):
            products[e, part * 8 : part * 8 + 8, :] = empty

    fetch.wait()

    def image(i, carry):
        for e in range(2):
            for k in range(count):
                row = idx[0, (e * half + i) * count + k]
                gathered[e, k : k + 1, :] = table_ref[row]
        for e in range(2):
            queries = [turned[0, t, pl.ds(e * half + i, 1), :] for t in range(8)]
            scales = [turned[1, t, pl.ds(e * half + i, 1), :] for t in range(8)]
            for part in range(padded // 8):
                near_ids, near_weights = spread(gathered[e, part * 8 : part * 8 + 8, :])
                acc = jnp.zeros_like(near_ids)
                for t in range(8):
                    acc = acc + jnp.where(near_ids == queries[t], scales[t], 0.0)
                at = pl.multiple_of(i * padded + part * 8, 8)
                products[e, pl.ds(at, 8), :] = acc * near_weights
        return carry

    lax.fori_loop(0, half, image, 0)
    for e in range(2):
        sums = lane_sums(products[e])
        for j in range(4):
            out_ref[e, j : j + 1, :] = sums[0:1, j * LANES : (j + 1) * LANES]
    if chosen is not None:
        store.wait()


def first_kernel(desc_ref, norm_ref, cross_ref, out):
    held = desc_ref.shape[0]
    out[0:held] = desc_ref[...]
    for e in range(2):
        out[held + e] = encode(norm_ref[2 * e : 2 * e + 2], cross_ref[e])


def merge_kernel(skip, recv, norm_ref, cross_ref, out, norm_out):
    kept = out.shape[0] - 2
    last = recv.shape[0] - 2
    out[0:kept] = recv[skip : skip + kept]
    for e in range(2):
        norms, dots, head = decode(recv[last + e])
        out[kept + e] = re_encode(head, dots + cross_ref[e])
        norm_out[2 * e : 2 * e + 2] = norm_ref[2 * e : 2 * e + 2] + norms


def trim_kernel(idx, recv_a, recv_b, norm_ref, cross_ref, out_a, out_b, norm_out):
    kept = out_a.shape[0]
    last = recv_b.shape[0] - 2
    for n in range(kept):
        out_a[n] = recv_a[idx[n]]
        out_b[n] = recv_b[idx[n]]
    for e in range(2):
        norms, dots, head = decode(recv_b[last + e])
        out_b[kept + e] = re_encode(head, dots + cross_ref[e])
        norm_out[2 * e : 2 * e + 2] = norm_ref[2 * e : 2 * e + 2] + norms


def tail_kernel(subs, info, *refs):
    blocks, (norm_ref, kept_ref, out) = refs[:-3], refs[-3:]
    core = info[0]
    last = len(blocks) // 2 - 1
    for j in range(last + 1):
        for q, src in ((core, blocks[2 * j]), (1 - core, blocks[2 * j + 1])):
            for s in range(subs):
                for c in range(2):
                    slot = 2 * s + c if j < last else 2 * (s % (subs // 2)) + c
                    out[s, 4 * j + 2 * c + q] = src[slot]
    recv = blocks[-1]
    size = recv.shape[0] - 2
    upward = core == 0
    totals = []
    empty = jnp.zeros((4, LANES), F32)
    for e in range(2):
        norms, dots, _ = decode(recv[size + e])
        totals.append(norm_ref[2 * e : 2 * e + 2] + jnp.where(upward, norms, 0.0))
        own = jnp.where(upward, dots, kept_ref[e])
        tile = jnp.concatenate(split3(own) + (empty,), axis=0).astype(BF16)
        for s in range(subs // 2):
            out[2 * s + e, 4 * last + 5] = tile
    tile = jnp.concatenate(split3(jnp.concatenate(totals, axis=0)) + (empty,), axis=0).astype(BF16)
    for s in range(subs):
        out[s, 4 * last + 4] = tile


def keep_kernel(recv, cross_ref, out):
    last = recv.shape[0] - 2
    for e in range(2):
        _, dots, _ = decode(recv[last + e])
        out[e] = dots + cross_ref[e]


def joined(tile):
    wide = tile.astype(F32)
    return (wide[0:4] + wide[4:8]) + wide[8:12]


def operands(plan, info, groups, pen, lhs, rhs, squares):
    subs = groups[0].shape[0]
    depth = groups[0].shape[2]
    row = lax.broadcasted_iota(I32, (depth, LANES), 0)
    ones = jnp.where(row < 4, 1.0, 0.0).astype(BF16)

    def prepare(slot, blocks):
        total = jnp.zeros((depth, LANES), F32)
        scaled = []
        for s, block in enumerate(blocks):
            rhs[slot, s * depth : (s + 1) * depth, :] = block
            value = block.astype(F32)
            scaled.append(value * -2.0)
            total = total + value * value
        square = jnp.sum(total, axis=0, keepdims=True)
        squares[pl.ds(slot, 1), :] = square
        parts = split3(square)
        extra = jnp.where(row == 0, parts[0], 0.0)
        extra = jnp.where(row == 1, parts[1], extra)
        extra = jnp.where(row == 2, parts[2], extra)
        scaled.append(jnp.where(row == 3, pen[pl.ds(slot, 1), :], extra))
        rhs[slot, subs * depth :, :] = ones
        lhs[slot] = jnp.concatenate(scaled, axis=0).T.astype(BF16)

    for which, first, positions, ways, at in plan:
        group = groups[which]

        def image(i, carry, group=group, first=first, ways=ways, at=at):
            if ways == 0:
                prepare(i, [group[s, at + i] for s in range(subs)])
                return carry
            source = i // 2
            step = source // ways
            lineage = source - ways * step if ways == 2 else info[2]
            tile = at + 4 * step + 2 * (i - 2 * source)
            prepare(2 * first + i, [group[2 * (s // 2) + lineage, tile + s % 2] for s in range(subs)])
            return carry

        lax.fori_loop(0, 2 * positions, image, 0)


def early_kernel(count, plan, info, *refs):
    pen, lhs, rhs, squares = refs[count:]
    operands(plan, info, refs[:count], pen, lhs, rhs, squares)


def joined(tile):
    wide = tile.astype(F32)
    return (wide[0:4] + wide[4:8]) + wide[8:12]


def match_kernel(plan, width, topk, padded, pairs, info, *refs):
    group, pen, live, near_row, near_lane, own_row, own_lane = refs[:7]
    nearest, margin, similarity, lhs, rhs, squares, least, less, query = refs[10:]
    pair_total = nearest.shape[0]
    subs = group.shape[0]
    end = group.shape[1]
    operands(plan, info, [group], pen, lhs, rhs, squares)

    near = jnp.zeros(near_row.shape, F32)
    own = jnp.zeros(near_row.shape, F32)
    for x in range(subs // 2):
        rows = joined(group[2 * x, end - 2]) + joined(group[2 * x + 1, end - 2])
        for h in range(4):
            line = jnp.broadcast_to(rows[h : h + 1], near_row.shape)
            at = jnp.take_along_axis(line, near_lane[...], axis=1)
            near = jnp.where(near_row[...] == 4 * x + h, at, near)
            at = jnp.take_along_axis(line, own_lane[...], axis=1)
            own = jnp.where(own_row[...] == 4 * x + h, at, own)
    chip = info[1]
    dots = joined(group[2 * chip, end - 1]) + joined(group[2 * chip + 1, end - 1])
    cosine = dots / jnp.sqrt(own * near)
    for r in range(similarity.shape[0]):
        line, lane = divmod(r * padded, LANES)
        both = jnp.concatenate((cosine[line : line + 1], cosine[line + 1 : line + 2]), axis=1) if line < 3 else cosine[3:4]
        similarity[r : r + 1, :] = both[:, lane : lane + topk]

    def pair(p, carry):
        asked = pairs[2 * p]
        refer = pairs[2 * p + 1]
        scores = jnp.dot(lhs[refer], rhs[asked], preferred_element_type=F32)
        first = scores[0:8]
        second = jnp.full_like(first, PENALTY)
        for b in range(1, LANES // 8):
            value = scores[8 * b : 8 * b + 8]
            second = jnp.minimum(second, jnp.maximum(first, value))
            first = jnp.minimum(first, value)
        least[p] = first
        less[p] = second
        query[pl.ds(p, 1), :] = squares[pl.ds(asked, 1), :]
        return carry

    def four(q, carry):
        for r in range(4):
            pair(4 * q + r, carry)
        return carry

    if pair_total % 4 == 0:
        lax.fori_loop(0, pair_total // 4, four, 0)
    else:
        lax.fori_loop(0, pair_total, pair, 0)
    first = least[:, 0, :]
    second = less[:, 0, :]
    for b in range(1, 8):
        other, runner = least[:, b, :], less[:, b, :]
        second = jnp.minimum(jnp.maximum(first, other), jnp.minimum(second, runner))
        first = jnp.minimum(first, other)
    alive = live[...] > 0.0
    nearest[...] = jnp.where(alive, (first + query[...]) * (1.0 / width), 0.0)
    margin[...] = jnp.where(alive, (second - first) * (1.0 / width), 0.0)


def local(word_ids, word_weights, neighbours, descriptors, keypoint_count, send_table, pair_slots):
    words = lax.axis_size("word")
    subs = lax.axis_size("sub")
    w = lax.axis_index("word")
    s = lax.axis_index("sub")
    core = lax.rem(s, 2)
    reach = words // 2
    pairs_of_ring = [
        (i * subs + j, ((i + (1 if j % 2 == 0 else words - 1)) % words) * subs + j)
        for i in range(words)
        for j in range(subs)
    ]
    _, images = word_ids.shape[1:]
    topk = neighbours.shape[0]
    padded = -(-topk // 8) * 8
    per = images // (words * subs)
    held, depth, points = descriptors.shape
    targets = 2 * subs
    width = depth * subs
    pair_total = pair_slots.shape[2]

    def send(x):
        return lax.ppermute(x, ("word", "sub"), pairs_of_ring)

    a = send(descriptors)
    partner = lax.ppermute(descriptors, "sub", [(j, j ^ 1) for j in range(subs)])

    chips = subs // 2
    chip = s // 2
    info = jnp.stack((core, chip, s // chips, w)).astype(I32)
    share = images // chips // LANES
    table, norm = call(
        table_kernel,
        (struct((images, LANES), F32), struct((share, LANES), F32)),
        (info, word_ids[0], word_weights[0]),
        [sm(), vm(), vm()],
        (),
        4,
    )
    table3 = table.reshape(images, 1, LANES)
    near = lax.dynamic_index_in_dim(neighbours.reshape(topk, words, chips, 2 * per), chip, 2, keepdims=False)
    near = jnp.transpose(near, (1, 2, 0)).reshape(words, 2 * per * topk)
    count = jnp.arange(1, reach + 1, dtype=I32)
    turn = lax.rem(w + jnp.where(core == 0, reach + 1 - count, reach + count), words)
    near_order = near[turn].reshape(reach, 1, 2 * per * topk)
    away = jnp.arange(0, reach, dtype=I32)
    taken_here = lax.dynamic_index_in_dim(send_table, w, 1, keepdims=False).reshape(words, targets)
    taken_mine = taken_here[lax.rem(w + jnp.where(core == 0, words - away, away), words)].reshape(-1)

    def cross(k, distance=None, sources=(), group=None, step=0, tiles=0):
        specs = [sm(), pl.BlockSpec(memory_space=pl.ANY), vm(), vm()]
        ins = [info, near_order, table3, table]
        outs = [struct((2, 4, LANES), F32)]
        chosen, aliases = None, {}
        if sources:
            chosen = (distance, step, len(sources) - 1, group is None)
            specs += [sm()]
            ins += [taken_mine, *sources]
            specs += [vm()] * len(sources)
            outs += [struct((subs, tiles, depth, points))]
            if group is not None:
                aliases = {len(ins): 1}
                ins += [group]
                specs += [pl.BlockSpec(memory_space=pl.ANY)]
        result = call(
            functools.partial(cross_kernel, topk, k, (reach + 1 - k, reach + k), words, chosen),
            outs,
            ins,
            specs,
            (
                pltpu.VMEM((2, 8, 2 * per, LANES), F32),
                pltpu.VMEM((2, padded, LANES), F32),
                pltpu.VMEM((2, 4 * LANES, LANES), F32),
                pltpu.SMEM((1, 2 * per * topk), I32),
                pltpu.SemaphoreType.DMA(()),
                pltpu.VMEM((subs, 4, depth, points), BF16),
                pltpu.SemaphoreType.DMA(()),
            ),
            4,
            aliases,
            {1},
        )
        return result if sources else result[0]

    order = [0]
    for d in range(1, reach):
        order += [words - d, d]
    order += [reach]
    source = lax.rem(w + jnp.array(order, I32), words)
    taken = taken_here[source]
    own_images = lax.dynamic_slice_in_dim(taken, 2 * s, 2, 1) + source[:, None] * held
    own_count = keypoint_count[own_images.reshape(-1)]
    column = jnp.arange(points, dtype=I32)[None, :]
    pen = jnp.where(column < own_count[:, None], 0.0, PENALTY).astype(F32)
    pairs = pair_slots[0, 0]
    delta = lax.rem(pairs // 2 - w + words, words)
    place = jnp.where(delta < reach, 2 * delta, 2 * (words - delta) - 1)
    pairs = place * 2 + lax.rem(pairs, 2)
    live = jnp.where(column < own_count[pairs[:, 0]][:, None], 1.0, 0.0).astype(F32)
    flat_pairs = pairs.reshape(-1)
    sign = 1 - 2 * core
    ahead = lax.rem(w + sign * jnp.arange(1, 5, dtype=I32) + words, words)
    behind = lax.rem(w - sign * (reach - 4) + words, words)
    trims = lax.dynamic_index_in_dim(send_table, behind, 0, keepdims=False).reshape(words, targets)[ahead]
    trims = jnp.concatenate((trims[:3].reshape(-1), lax.dynamic_slice_in_dim(trims[3], core * subs, subs, 0)))

    at_own = (w * subs + s) * per
    listed = jnp.transpose(lax.dynamic_slice_in_dim(neighbours, at_own, per, 1), (1, 0))
    listed = jnp.pad(listed, ((0, 0), (0, padded - topk)))
    itself = at_own + jnp.arange(per, dtype=I32)[:, None] + jnp.zeros((1, padded), I32)

    def locate(image):
        flat = jnp.pad(image.reshape(-1), (0, 4 * LANES - per * padded)).reshape(4, LANES)
        return flat // LANES, lax.rem(flat, LANES)

    near_row, near_lane = locate(listed)
    own_row, own_lane = locate(itself)

    norm_struct = struct((share, LANES), F32)
    first = (partner, norm, cross(1))
    b = send(call(first_kernel, struct((held + 2, depth, points)), first))
    norm = jnp.where(core == 0, norm, 0.0)
    full = reach - 4
    cut = GROUPS[0]
    blocks = [(descriptors,), (a, b)]
    group = None
    exchange = []
    plan = [(0, 1, 2 * cut, 2, 0), (0, 0, 1, 0, 4 * cut), (1, 2 * cut + 1, 2 * (full - cut), 2, 0)]

    def step(k):
        nonlocal group
        d = k - 2
        if d > full:
            return cross(k)
        if d == 0:
            where, tiles = 4 * cut, 4 * cut + 2
        elif d <= cut:
            where, tiles = 4 * (d - 1), 4 * cut + 2
        else:
            where, tiles = 4 * (d - 1 - cut), 4 * (full - cut)
        product, group = cross(k, d, blocks[d], group, where, tiles)
        if d in (cut, full):
            exchange.append(lax.all_to_all(group, "sub", 0, 0, tiled=True))
            group = None
        return product

    for k in range(2, full + 1):
        product = step(k)
        a = send(a)
        merged, norm = call(
            functools.partial(merge_kernel, 0), (struct((held + 2, depth, points)), norm_struct), (b, norm, product)
        )
        b = send(merged)
        blocks.append((a, b))
    size = 3 * targets + subs
    a, b, norm = call(
        trim_kernel,
        (struct((size, depth, points)), struct((size + 2, depth, points)), norm_struct),
        (trims, a, b, norm, step(full + 1)),
        [sm()] + [vm()] * 4,
    )
    a, b = send(a), send(b)
    last = [a, b]
    for k in range(full + 2, reach + 1):
        size -= targets
        product = step(k)
        if k == reach:
            kept = call(keep_kernel, struct((2, 4, LANES), F32), (b, product))
        a = send(a[targets:])
        merged, norm = call(
            functools.partial(merge_kernel, targets),
            (struct((size + 2, depth, points)), norm_struct),
            (b, norm, product),
        )
        b = send(merged)
        last += [a, b]
    steps = len(last) // 2
    tail = call(
        functools.partial(tail_kernel, subs),
        struct((subs, 4 * steps + 2, depth, points)),
        (info, *last, norm, kept),
        [sm()] + [vm()] * (len(last) + 2),
    )
    tail = lax.all_to_all(tail, "sub", 0, 0, tiled=True)

    total = 2 * words
    held_struct = (
        struct((total, points, width + depth)),
        struct((total, width + depth, points)),
        struct((total, points), F32),
    )
    ready = call(
        functools.partial(early_kernel, len(exchange), plan),
        held_struct,
        (info, *exchange, pen),
        [sm()] + [vm()] * (len(exchange) + 1),
    )
    plan = [(0, 2 * full + 1, 2 * (steps - 1), 2, 0), (0, 2 * reach - 1, 1, 1, 4 * (steps - 1))]
    ins = (flat_pairs, info, tail, pen, live, near_row, near_lane, own_row, own_lane, *ready)
    rows = struct((pair_total, points), F32)
    nearest, margin, similarity, *_ = call(
        functools.partial(match_kernel, plan, width, topk, padded),
        (rows, rows, struct((per, topk), F32), *held_struct),
        ins,
        [sm(), sm()] + [vm()] * (len(ins) - 2),
        (
            pltpu.VMEM((pair_total, 8, points), F32),
            pltpu.VMEM((pair_total, 8, points), F32),
            pltpu.VMEM((pair_total, points), F32),
        ),
        4,
        {9: 3, 10: 4, 11: 5},
    )
    return similarity, nearest[None, None], margin[None, None]


def solution(mesh):
    in_specs = (
        P("word", None, "groups"),
        P("word", None, "groups"),
        P(None, "groups"),
        P(("groups", "word"), "sub", None),
        P("groups"),
        P("groups", None, None, None),
        P(("groups", "word"), "sub", None, None),
    )
    out_specs = (
        P(("groups", "word", "sub"), None),
        P(("groups", "word"), "sub", None, None),
        P(("groups", "word"), "sub", None, None),
    )

    return jax.shard_map(local, mesh=mesh, in_specs=in_specs, out_specs=out_specs, check_vma=False)
```

time: 337 us -> 277 us (0.82)
  waiting for transfers between devices: 105 us -> 32.7 us
  starting transfers between devices: 95.4 us -> 134 us
  Pallas kernels: 82.1 us -> 68.8 us
  local copies, waits for them, and re-layouts: 42.7 us -> 30.2 us
    ppermute x32, waiting for transfers between devices: 96.3 us -> 32.7 us  [send(): return lax.ppermute(x, ('word', 'sub'), pairs_of_ring)]
    ppermute x1, starting transfers between devices: 2.08 us -> 42.2 us  [local(): lax.ppermute(descriptors, 'sub', [(j, j ^ 1) for j in range(subs)])]
    pallas_call x38 -> x37, Pallas kernels: 82.1 us -> 68.8 us  [call(): pl.pallas_call(body, out_shape=[x if INTERPRET or i in outside else VMEM(...]
    unnamed x98 -> x66, local copies, waits for them, and re-layouts: 27.3 us -> 15.7 us
    all_to_all x3, waiting for transfers between devices: 8.78 us -> 0.01 us  [the longest x2 0.01 us: step(): exchange.append(lax.all_to_all(group, 'sub', 0, 0, tiled=True))]
  transfers between devices with their start and end apart: 36 -> 36, of which waited for: 16 -> 20; matrix products, arithmetic and copies ran while one was open for 8% -> 9% of each run, Pallas kernels for 21% -> 23%
where the time goes in v1:
time: 277 us; the launch traced here: 274 us
  starting transfers between devices  134 us (48%)
  Pallas kernels  68.8 us (25%)
  waiting for transfers between devices  32.7 us (12%)
  local copies, waits for them, and re-layouts  30.2 us (11%)
  other arithmetic  6.45 us (2%)
    ppermute x32, starting transfers between devices, send(): return lax.ppermute(x, ('word', 'sub'), pairs_of_ring)  71.7 us
    pallas_call x37, Pallas kernels, call(): pl.pallas_call(body, out_shape=[x if INTERPRET or i in outside else VMEM(...  68.8 us
    ppermute x1, starting transfers between devices, local(): lax.ppermute(descriptors, 'sub', [(j, j ^ 1) for j in range(subs)])  42.2 us
    ppermute x32, waiting for transfers between devices, send(): return lax.ppermute(x, ('word', 'sub'), pairs_of_ring)  32.7 us
    all_to_all x2, starting transfers between devices, step(): exchange.append(lax.all_to_all(group, 'sub', 0, 0, tiled=True))  15.8 us
    unnamed x66, local copies, waits for them, and re-layouts  15.7 us
  transfers between devices with their start and end apart: 36, of which 20 were waited for; matrix products, arithmetic and copies ran while one was open for 9% of the time, Pallas kernels for 23%

profile of v1, /device:TPU:38, one launch (start us, length us, event | category | flops | bytes accessed | tf_op | source)
XLA Modules:
  0.0 274.2 jit_solution(9593178402408075537)
XLA Ops:
  0.6 4.8 %collective-permute-start = (bf16[64,16,128]{2,1,0:T(8,128)(2,1)}, bf16[64,16,128]{2,1,0:T(8,128)(2,1)S(1)}, u32[]{:S(2)}, u32[]{:S(2)}) collective-permute-start(bf16[64,16,128]{2,1,0:T(8,128)(2,1)} %refs_1_.1), channel_id=1, source_target_pairs={{0,8},{1,249},{2,10},{3,251},{4,12},{5,253},{6,14},{7,255},{8,16},... | collective-permute-start | bytes 786440 | tf_op jit(solution)/shard_map/ppermute | solution.py:393
  5.5 42.2 %collective-permute-start.12 = (bf16[64,16,128]{2,1,0:T(8,128)(2,1)}, bf16[64,16,128]{2,1,0:T(8,128)(2,1)S(1)}, u32[]{:S(2)}, u32[]{:S(2)}) collective-permute-start(bf16[64,16,128]{2,1,0:T(8,128)(2,1)} %refs_1_.1), channel_id=1, source_target_pairs={{0,1},{1,0},{2,3},{3,2},{4,5},{5,4},{6,7},{7,6},{8,9},{9,8},{10,11... | collective-permute-start | bytes 786440 | tf_op jit(solution)/shard_map/ppermute | solution.py:396
  57.4 3.1 %shard_map.106 = (f32[2,4,128]{2,1,0:T(4,128)S(1)}, bf16[8,34,16,128]{3,2,1,0:T(8,128)(2,1)}) custom-call(s32[4]{0:T(128)S(1)} %pad_add_fusion.info, s32[16,1,800]{2,1,0:T(1,128)S(1)} %reshape.226.lists, f32[2048,1,128]{2,1,0:T(1,128)S(1)} %bitcast.90, f32[2048,128]{1,0:T(8,128)S(1)} %get-tuple-element.69.rows_ref, s32[256]{0:T(256)S(1)} %reshape.229.refs_0_, ...), custom_call_target="tpu_custom_call" | custom-call | tf_op jit(solution)/shard_map/pallas_call | solution.py:29
  60.5 3.5 %collective-permute-done.13.recv.refs_2_ = bf16[66,16,128]{2,1,0:T(8,128)(2,1)S(1)} collective-permute-done((bf16[66,16,128]{2,1,0:T(8,128)(2,1)S(1)}, bf16[66,16,128]{2,1,0:T(8,128)(2,1)S(1)}, u32[]{:S(2)}, u32[]{:S(2)}) %collective-permute-start.13) | collective-permute-done | bytes 270368 | tf_op jit(solution)/shard_map/ppermute | solution.py:393
  68.0 3.1 %shard_map.108 = (f32[2,4,128]{2,1,0:T(4,128)S(1)}, bf16[8,34,16,128]{3,2,1,0:T(8,128)(2,1)}) custom-call(s32[4]{0:T(128)S(1)} %pad_add_fusion.info, s32[16,1,800]{2,1,0:T(1,128)S(1)} %reshape.226.lists, f32[2048,1,128]{2,1,0:T(1,128)S(1)} %bitcast.91, f32[2048,128]{1,0:T(8,128)S(1)} %get-tuple-element.69.rows_ref, ...), custom_call_target="tpu_custom_call", output_to_operand_aliasing={{1}: (7, {})} | custom-call | tf_op jit(solution)/shard_map/pallas_call | solution.py:29
  78.4 3.1 %shard_map.110 = (f32[2,4,128]{2,1,0:T(4,128)S(1)}, bf16[8,34,16,128]{3,2,1,0:T(8,128)(2,1)}) custom-call(s32[4]{0:T(128)S(1)} %pad_add_fusion.info, s32[16,1,800]{2,1,0:T(1,128)S(1)} %reshape.226.lists, f32[2048,1,128]{2,1,0:T(1,128)S(1)} %bitcast.92, f32[2048,128]{1,0:T(8,128)S(1)} %get-tuple-element.69.rows_ref, ...), custom_call_target="tpu_custom_call", output_to_operand_aliasing={{1}: (7, {})} | custom-call | tf_op jit(solution)/shard_map/pallas_call | solution.py:29
  88.1 3.1 %shard_map.112 = (f32[2,4,128]{2,1,0:T(4,128)S(1)}, bf16[8,34,16,128]{3,2,1,0:T(8,128)(2,1)}) custom-call(s32[4]{0:T(128)S(1)} %pad_add_fusion.info, s32[16,1,800]{2,1,0:T(1,128)S(1)} %reshape.226.lists, f32[2048,1,128]{2,1,0:T(1,128)S(1)} %bitcast.93, f32[2048,128]{1,0:T(8,128)S(1)} %get-tuple-element.69.rows_ref, ...), custom_call_target="tpu_custom_call", output_to_operand_aliasing={{1}: (7, {})} | custom-call | tf_op jit(solution)/shard_map/pallas_call | solution.py:29
  97.7 3.1 %shard_map.114 = (f32[2,4,128]{2,1,0:T(4,128)S(1)}, bf16[8,34,16,128]{3,2,1,0:T(8,128)(2,1)}) custom-call(s32[4]{0:T(128)S(1)} %pad_add_fusion.info, s32[16,1,800]{2,1,0:T(1,128)S(1)} %reshape.226.lists, f32[2048,1,128]{2,1,0:T(1,128)S(1)} %bitcast.94, f32[2048,128]{1,0:T(8,128)S(1)} %get-tuple-element.69.rows_ref, ...), custom_call_target="tpu_custom_call", output_to_operand_aliasing={{1}: (7, {})} | custom-call | tf_op jit(solution)/shard_map/pallas_call | solution.py:29
  107.3 3.1 %shard_map.116 = (f32[2,4,128]{2,1,0:T(4,128)S(1)}, bf16[8,34,16,128]{3,2,1,0:T(8,128)(2,1)}) custom-call(s32[4]{0:T(128)S(1)} %pad_add_fusion.info, s32[16,1,800]{2,1,0:T(1,128)S(1)} %reshape.226.lists, f32[2048,1,128]{2,1,0:T(1,128)S(1)} %bitcast.95, f32[2048,128]{1,0:T(8,128)S(1)} %get-tuple-element.69.rows_ref, ...), custom_call_target="tpu_custom_call", output_to_operand_aliasing={{1}: (7, {})} | custom-call | tf_op jit(solution)/shard_map/pallas_call | solution.py:29
  117.0 7.6 %collective-permute-done.6.refs_1_ = bf16[64,16,128]{2,1,0:T(8,128)(2,1)S(1)} collective-permute-done((bf16[64,16,128]{2,1,0:T(8,128)(2,1)S(1)}, bf16[64,16,128]{2,1,0:T(8,128)(2,1)S(1)}, u32[]{:S(2)}, u32[]{:S(2)}) %collective-permute-start.6) | collective-permute-done | bytes 262176 | tf_op jit(solution)/shard_map/ppermute | solution.py:393
  126.6 3.1 %shard_map.118 = (f32[2,4,128]{2,1,0:T(4,128)S(1)}, bf16[8,34,16,128]{3,2,1,0:T(8,128)(2,1)}) custom-call(s32[4]{0:T(128)S(1)} %pad_add_fusion.info, s32[16,1,800]{2,1,0:T(1,128)S(1)} %reshape.226.lists, f32[2048,1,128]{2,1,0:T(1,128)S(1)} %bitcast.96, f32[2048,128]{1,0:T(8,128)S(1)} %get-tuple-element.69.rows_ref, ...), custom_call_target="tpu_custom_call", output_to_operand_aliasing={{1}: (7, {})} | custom-call | tf_op jit(solution)/shard_map/pallas_call | solution.py:29
  136.1 3.1 %shard_map.120 = (f32[2,4,128]{2,1,0:T(4,128)S(1)}, bf16[8,34,16,128]{3,2,1,0:T(8,128)(2,1)}) custom-call(s32[4]{0:T(128)S(1)} %pad_add_fusion.info, s32[16,1,800]{2,1,0:T(1,128)S(1)} %reshape.226.lists, f32[2048,1,128]{2,1,0:T(1,128)S(1)} %bitcast.97, f32[2048,128]{1,0:T(8,128)S(1)} %get-tuple-element.69.rows_ref, ...), custom_call_target="tpu_custom_call", output_to_operand_aliasing={{1}: (7, {})} | custom-call | tf_op jit(solution)/shard_map/pallas_call | solution.py:29
  145.6 3.1 %shard_map.122 = (f32[2,4,128]{2,1,0:T(4,128)S(1)}, bf16[8,34,16,128]{3,2,1,0:T(8,128)(2,1)}) custom-call(s32[4]{0:T(128)S(1)} %pad_add_fusion.info, s32[16,1,800]{2,1,0:T(1,128)S(1)} %reshape.226.lists, f32[2048,1,128]{2,1,0:T(1,128)S(1)} %bitcast.98, f32[2048,128]{1,0:T(8,128)S(1)} %get-tuple-element.69.rows_ref, ...), custom_call_target="tpu_custom_call", output_to_operand_aliasing={{1}: (7, {})} | custom-call | tf_op jit(solution)/shard_map/pallas_call | solution.py:29
  152.8 4.7 %all-to-all-start.1 = ((bf16[8,34,16,128]{3,2,1,0:T(8,128)(2,1)}), bf16[8,34,16,128]{3,2,1,0:T(8,128)(2,1)S(1)}, u32[]{:S(2)}, u32[]{:S(2)}) async-start(bf16[8,34,16,128]{3,2,1,0:T(8,128)(2,1)} %get-tuple-element.125), calls=%async_computation.1 | async-start | bytes 2228224 | tf_op jit(solution)/shard_map/all_to_all | solution.py:513
  161.6 3.1 %shard_map.124 = (f32[2,4,128]{2,1,0:T(4,128)S(1)}, bf16[8,16,16,128]{3,2,1,0:T(8,128)(2,1)}) custom-call(s32[4]{0:T(128)S(1)} %pad_add_fusion.info, s32[16,1,800]{2,1,0:T(1,128)S(1)} %reshape.226.lists, f32[2048,1,128]{2,1,0:T(1,128)S(1)} %bitcast.99, f32[2048,128]{1,0:T(8,128)S(1)} %get-tuple-element.69.rows_ref, s32[256]{0:T(256)S(1)} %reshape.229.refs_0_, ...), custom_call_target="tpu_custom_call" | custom-call | tf_op jit(solution)/shard_map/pallas_call | solution.py:29
  174.0 3.1 %shard_map.126 = (f32[2,4,128]{2,1,0:T(4,128)S(1)}, bf16[8,16,16,128]{3,2,1,0:T(8,128)(2,1)}) custom-call(s32[4]{0:T(128)S(1)} %pad_add_fusion.info, s32[16,1,800]{2,1,0:T(1,128)S(1)} %reshape.226.lists, f32[2048,1,128]{2,1,0:T(1,128)S(1)} %bitcast.100, f32[2048,128]{1,0:T(8,128)S(1)} %get-tuple-element.69.rows_ref, ...), custom_call_target="tpu_custom_call", output_to_operand_aliasing={{1}: (7, {})} | custom-call | tf_op jit(solution)/shard_map/pallas_call | solution.py:29
  187.3 3.1 %shard_map.128 = (f32[2,4,128]{2,1,0:T(4,128)S(1)}, bf16[8,16,16,128]{3,2,1,0:T(8,128)(2,1)}) custom-call(s32[4]{0:T(128)S(1)} %pad_add_fusion.info, s32[16,1,800]{2,1,0:T(1,128)S(1)} %reshape.226.lists, f32[2048,1,128]{2,1,0:T(1,128)S(1)} %bitcast.101, f32[2048,128]{1,0:T(8,128)S(1)} %get-tuple-element.69.rows_ref, ...), custom_call_target="tpu_custom_call", output_to_operand_aliasing={{1}: (7, {})} | custom-call | tf_op jit(solution)/shard_map/pallas_call | solution.py:29
  194.2 5.2 %collective-permute-start.26 = (bf16[58,16,128]{2,1,0:T(8,128)(2,1)}, bf16[58,16,128]{2,1,0:T(8,128)(2,1)S(1)}, u32[]{:S(2)}, u32[]{:S(2)}) collective-permute-start(bf16[58,16,128]{2,1,0:T(8,128)(2,1)} %get-tuple-element.115), channel_id=1, source_target_pairs={{0,8},{1,249},{2,10},{3,251},{4,12},{5,253},{6,14},{7,255},{8,16},... | collective-permute-start | bytes 712712 | tf_op jit(solution)/shard_map/ppermute | solution.py:393
  200.2 3.1 %shard_map.130 = (f32[2,4,128]{2,1,0:T(4,128)S(1)}, bf16[8,16,16,128]{3,2,1,0:T(8,128)(2,1)}) custom-call(s32[4]{0:T(128)S(1)} %pad_add_fusion.info, s32[16,1,800]{2,1,0:T(1,128)S(1)} %reshape.226.lists, f32[2048,1,128]{2,1,0:T(1,128)S(1)} %bitcast.102, f32[2048,128]{1,0:T(8,128)S(1)} %get-tuple-element.69.rows_ref, ...), custom_call_target="tpu_custom_call", output_to_operand_aliasing={{1}: (7, {})} | custom-call | tf_op jit(solution)/shard_map/pallas_call | solution.py:29
  203.4 11.1 %all-to-all-start.2 = ((bf16[8,16,16,128]{3,2,1,0:T(8,128)(2,1)}), bf16[8,16,16,128]{3,2,1,0:T(8,128)(2,1)S(1)}, u32[]{:S(2)}, u32[]{:S(2)}) async-start(bf16[8,16,16,128]{3,2,1,0:T(8,128)(2,1)} %get-tuple-element.126), calls=%async_computation.2 | async-start | bytes 1048576 | tf_op jit(solution)/shard_map/all_to_all | solution.py:513
  231.1 3.6 %collective-permute-start.30 = (bf16[26,16,128]{2,1,0:T(8,128)(2,1)S(1)}, bf16[26,16,128]{2,1,0:T(8,128)(2,1)S(1)}, u32[]{:S(2)}, u32[]{:S(2)}) collective-permute-start(bf16[26,16,128]{2,1,0:T(8,128)(2,1)S(1)} %get-tuple-element.121), channel_id=1, source_target_pairs={{0,8},{1,249},{2,10},{3,251},{4,12},{5,253},{6,14},{7,255},{8,16},... | collective-permute-start | bytes 319496 | tf_op jit(solution)/shard_map/ppermute | solution.py:393
  248.1 4.8 %all-to-all-start = ((bf16[8,18,16,128]{3,2,1,0:T(8,128)(2,1)}), bf16[8,18,16,128]{3,2,1,0:T(8,128)(2,1)S(1)}, u32[]{:S(2)}, u32[]{:S(2)}) async-start(bf16[8,18,16,128]{3,2,1,0:T(8,128)(2,1)} %shard_map.137), calls=%async_computation | async-start | bytes 1179648 | tf_op jit(solution)/shard_map/all_to_all | solution.py:554
  253.0 7.4 %shard_map.138 = (bf16[64,128,144]{2,1,0:T(8,128)(2,1)S(1)}, bf16[64,144,128]{2,1,0:T(8,128)(2,1)S(1)}, f32[64,128]{1,0:T(8,128)S(1)}) custom-call(s32[4]{0:T(128)S(1)} %pad_add_fusion.info, bf16[8,34,16,128]{3,2,1,0:T(8,128)(2,1)S(1)} %all-to-all-done.1.refs_0_, bf16[8,16,16,128]{3,2,1,0:T(8,128)(2,1)S(1)} %all-to-all-done.2.refs_1_, ...), custom_call_target="tpu_custom_call" | custom-call | tf_op jit(solution)/shard_map/pallas_call | solution.py:29
  267.7 4.6 %shard_map.139 = (f32[32,128]{1,0:T(8,128)S(1)}, f32[32,128]{1,0:T(8,128)S(1)}, f32[8,50]{1,0:T(8,128)S(1)}, bf16[64,128,144]{2,1,0:T(8,128)(2,1)S(1)}, bf16[64,...) custom-call(s32[64]{0:T(128)S(1)} %fusion.14.pairs, ...), custom_call_target="tpu_custom_call", output_to_operand_aliasing={{3}: (9, {}), {4}: (10, {}), {5}: (11, {})} | custom-call | tf_op jit(solution)/shard_map/pallas_call | solution.py:29
  (201 shorter events, 132.5 us)
Async XLA Ops:
  0.6 65.4 %collective-permute-start = (bf16[64,16,128]{2,1,0:T(8,128)(2,1)}, bf16[64,16,128]{2,1,0:T(8,128)(2,1)S(1)}, u32[]{:S(2)}, u32[]{:S(2)}) collective-permute-start(bf16[64,16,128]{2,1,0:T(8,128)(2,1)} %refs_1_.1), channel_id=1, source_target_pairs={{0,8},{1,249},{2,10},{3,251},{4,12},{5,253},{6,14},{7,255},{8,16},... | collective-permute-start | bytes 786440 | tf_op jit(solution)/shard_map/ppermute | solution.py:393
  5.5 48.9 %collective-permute-start.12 = (bf16[64,16,128]{2,1,0:T(8,128)(2,1)}, bf16[64,16,128]{2,1,0:T(8,128)(2,1)S(1)}, u32[]{:S(2)}, u32[]{:S(2)}) collective-permute-start(bf16[64,16,128]{2,1,0:T(8,128)(2,1)} %refs_1_.1), channel_id=1, source_target_pairs={{0,1},{1,0},{2,3},{3,2},{4,5},{5,4},{6,7},{7,6},{8,9},{9,8},{10,11... | collective-permute-start | bytes 786440 | tf_op jit(solution)/shard_map/ppermute | solution.py:396
  54.4 9.6 %collective-permute-start.13 = (bf16[66,16,128]{2,1,0:T(8,128)(2,1)S(1)}, bf16[66,16,128]{2,1,0:T(8,128)(2,1)S(1)}, u32[]{:S(2)}, u32[]{:S(2)}) collective-permute-start(bf16[66,16,128]{2,1,0:T(8,128)(2,1)S(1)} %shard_map.105), channel_id=1, source_target_pairs={{0,8},{1,249},{2,10},{3,251},{4,12},{5,253},{6,14},{7,255},{8,16},... | collective-permute-start | bytes 811016 | tf_op jit(solution)/shard_map/ppermute | solution.py:393
  66.0 10.4 %collective-permute-start.1 = (bf16[64,16,128]{2,1,0:T(8,128)(2,1)S(1)}, bf16[64,16,128]{2,1,0:T(8,128)(2,1)S(1)}, u32[]{:S(2)}, u32[]{:S(2)}) collective-permute-start(bf16[64,16,128]{2,1,0:T(8,128)(2,1)S(1)} %collective-permute-done.refs_1_), channel_id=1, source_target_pairs={{0,8},{1,249},{2,10},{3,251},{4,12},{5,253},{6,14},{7,255},{8,16},... | collective-permute-start | bytes 786440 | tf_op jit(solution)/shard_map/ppermute | solution.py:393
  76.5 9.6 %collective-permute-start.2 = (bf16[64,16,128]{2,1,0:T(8,128)(2,1)S(1)}, bf16[64,16,128]{2,1,0:T(8,128)(2,1)S(1)}, u32[]{:S(2)}, u32[]{:S(2)}) collective-permute-start(bf16[64,16,128]{2,1,0:T(8,128)(2,1)S(1)} %collective-permute-done.1.refs_1_), channel_id=1, source_target_pairs={{0,8},{1,249},{2,10},{3,251},{4,12},{5,253},{6,14},{7,255},{8,16},... | collective-permute-start | bytes 786440 | tf_op jit(solution)/shard_map/ppermute | solution.py:393
  83.3 9.6 %collective-permute-start.16 = (bf16[66,16,128]{2,1,0:T(8,128)(2,1)S(1)}, bf16[66,16,128]{2,1,0:T(8,128)(2,1)S(1)}, u32[]{:S(2)}, u32[]{:S(2)}) collective-permute-start(bf16[66,16,128]{2,1,0:T(8,128)(2,1)S(1)} %get-tuple-element.79), channel_id=1, source_target_pairs={{0,8},{1,249},{2,10},{3,251},{4,12},{5,253},{6,14},{7,255},{8,16},... | collective-permute-start | bytes 811016 | tf_op jit(solution)/shard_map/ppermute | solution.py:393
  86.1 9.6 %collective-permute-start.3 = (bf16[64,16,128]{2,1,0:T(8,128)(2,1)S(1)}, bf16[64,16,128]{2,1,0:T(8,128)(2,1)S(1)}, u32[]{:S(2)}, u32[]{:S(2)}) collective-permute-start(bf16[64,16,128]{2,1,0:T(8,128)(2,1)S(1)} %collective-permute-done.2.refs_1_), channel_id=1, source_target_pairs={{0,8},{1,249},{2,10},{3,251},{4,12},{5,253},{6,14},{7,255},{8,16},... | collective-permute-start | bytes 786440 | tf_op jit(solution)/shard_map/ppermute | solution.py:393
  95.7 9.6 %collective-permute-start.4 = (bf16[64,16,128]{2,1,0:T(8,128)(2,1)S(1)}, bf16[64,16,128]{2,1,0:T(8,128)(2,1)S(1)}, u32[]{:S(2)}, u32[]{:S(2)}) collective-permute-start(bf16[64,16,128]{2,1,0:T(8,128)(2,1)S(1)} %collective-permute-done.3.refs_1_), channel_id=1, source_target_pairs={{0,8},{1,249},{2,10},{3,251},{4,12},{5,253},{6,14},{7,255},{8,16},... | collective-permute-start | bytes 786440 | tf_op jit(solution)/shard_map/ppermute | solution.py:393
  105.4 9.6 %collective-permute-start.5 = (bf16[64,16,128]{2,1,0:T(8,128)(2,1)S(1)}, bf16[64,16,128]{2,1,0:T(8,128)(2,1)S(1)}, u32[]{:S(2)}, u32[]{:S(2)}) collective-permute-start(bf16[64,16,128]{2,1,0:T(8,128)(2,1)S(1)} %collective-permute-done.4.refs_1_), channel_id=1, source_target_pairs={{0,8},{1,249},{2,10},{3,251},{4,12},{5,253},{6,14},{7,255},{8,16},... | collective-permute-start | bytes 786440 | tf_op jit(solution)/shard_map/ppermute | solution.py:393
  112.2 17.5 %collective-permute-start.19 = (bf16[66,16,128]{2,1,0:T(8,128)(2,1)S(1)}, bf16[66,16,128]{2,1,0:T(8,128)(2,1)S(1)}, u32[]{:S(2)}, u32[]{:S(2)}) collective-permute-start(bf16[66,16,128]{2,1,0:T(8,128)(2,1)S(1)} %get-tuple-element.91), channel_id=1, source_target_pairs={{0,8},{1,249},{2,10},{3,251},{4,12},{5,253},{6,14},{7,255},{8,16},... | collective-permute-start | bytes 811016 | tf_op jit(solution)/shard_map/ppermute | solution.py:393
  115.0 9.6 %collective-permute-start.6 = (bf16[64,16,128]{2,1,0:T(8,128)(2,1)S(1)}, bf16[64,16,128]{2,1,0:T(8,128)(2,1)S(1)}, u32[]{:S(2)}, u32[]{:S(2)}) collective-permute-start(bf16[64,16,128]{2,1,0:T(8,128)(2,1)S(1)} %collective-permute-done.5.refs_1_), channel_id=1, source_target_pairs={{0,8},{1,249},{2,10},{3,251},{4,12},{5,253},{6,14},{7,255},{8,16},... | collective-permute-start | bytes 786440 | tf_op jit(solution)/shard_map/ppermute | solution.py:393
  143.6 15.0 %collective-permute-start.9 = (bf16[64,16,128]{2,1,0:T(8,128)(2,1)S(1)}, bf16[64,16,128]{2,1,0:T(8,128)(2,1)S(1)}, u32[]{:S(2)}, u32[]{:S(2)}) collective-permute-start(bf16[64,16,128]{2,1,0:T(8,128)(2,1)S(1)} %collective-permute-done.8.refs_1_), channel_id=1, source_target_pairs={{0,8},{1,249},{2,10},{3,251},{4,12},{5,253},{6,14},{7,255},{8,16},... | collective-permute-start | bytes 786440 | tf_op jit(solution)/shard_map/ppermute | solution.py:393
  150.3 14.4 %collective-permute-start.22 = (bf16[66,16,128]{2,1,0:T(8,128)(2,1)}, bf16[66,16,128]{2,1,0:T(8,128)(2,1)S(1)}, u32[]{:S(2)}, u32[]{:S(2)}) collective-permute-start(bf16[66,16,128]{2,1,0:T(8,128)(2,1)} %get-tuple-element.103), channel_id=1, source_target_pairs={{0,8},{1,249},{2,10},{3,251},{4,12},{5,253},{6,14},{7,255},{8,16},... | collective-permute-start | bytes 811016 | tf_op jit(solution)/shard_map/ppermute | solution.py:393
  152.8 50.6 %all-to-all-start.1 = ((bf16[8,34,16,128]{3,2,1,0:T(8,128)(2,1)}), bf16[8,34,16,128]{3,2,1,0:T(8,128)(2,1)S(1)}, u32[]{:S(2)}, u32[]{:S(2)}) async-start(bf16[8,34,16,128]{3,2,1,0:T(8,128)(2,1)} %get-tuple-element.125), calls=%async_computation.1 | async-start | bytes 2228224 | tf_op jit(solution)/shard_map/all_to_all | solution.py:513
  158.7 12.4 %collective-permute-start.10 = (bf16[64,16,128]{2,1,0:T(8,128)(2,1)S(1)}, bf16[64,16,128]{2,1,0:T(8,128)(2,1)S(1)}, u32[]{:S(2)}, u32[]{:S(2)}) collective-permute-start(bf16[64,16,128]{2,1,0:T(8,128)(2,1)S(1)} %collective-permute-done.9.refs_1_), channel_id=1, source_target_pairs={{0,8},{1,249},{2,10},{3,251},{4,12},{5,253},{6,14},{7,255},{8,16},... | collective-permute-start | bytes 786440 | tf_op jit(solution)/shard_map/ppermute | solution.py:393
  166.0 11.1 %collective-permute-start.23 = (bf16[66,16,128]{2,1,0:T(8,128)(2,1)}, bf16[66,16,128]{2,1,0:T(8,128)(2,1)S(1)}, u32[]{:S(2)}, u32[]{:S(2)}) collective-permute-start(bf16[66,16,128]{2,1,0:T(8,128)(2,1)} %get-tuple-element.106), channel_id=1, source_target_pairs={{0,8},{1,249},{2,10},{3,251},{4,12},{5,253},{6,14},{7,255},{8,16},... | collective-permute-start | bytes 811016 | tf_op jit(solution)/shard_map/ppermute | solution.py:393
  171.1 19.3 %collective-permute-start.11 = (bf16[64,16,128]{2,1,0:T(8,128)(2,1)S(1)}, bf16[64,16,128]{2,1,0:T(8,128)(2,1)S(1)}, u32[]{:S(2)}, u32[]{:S(2)}) collective-permute-start(bf16[64,16,128]{2,1,0:T(8,128)(2,1)S(1)} %collective-permute-done.10.refs_1_), channel_id=1, source_target_pairs={{0,8},{1,249},{2,10},{3,251},{4,12},{5,253},{6,14},{7,255},{8,16},... | collective-permute-start | bytes 786440 | tf_op jit(solution)/shard_map/ppermute | solution.py:393
  178.5 11.9 %collective-permute-start.24 = (bf16[66,16,128]{2,1,0:T(8,128)(2,1)}, bf16[66,16,128]{2,1,0:T(8,128)(2,1)S(1)}, u32[]{:S(2)}, u32[]{:S(2)}) collective-permute-start(bf16[66,16,128]{2,1,0:T(8,128)(2,1)} %get-tuple-element.110), channel_id=1, source_target_pairs={{0,8},{1,249},{2,10},{3,251},{4,12},{5,253},{6,14},{7,255},{8,16},... | collective-permute-start | bytes 811016 | tf_op jit(solution)/shard_map/ppermute | solution.py:393
  191.8 22.7 %collective-permute-start.25 = (bf16[56,16,128]{2,1,0:T(8,128)(2,1)}, bf16[56,16,128]{2,1,0:T(8,128)(2,1)}, u32[]{:S(2)}, u32[]{:S(2)}) collective-permute-start(bf16[56,16,128]{2,1,0:T(8,128)(2,1)} %get-tuple-element.114), channel_id=1, source_target_pairs={{0,8},{1,249},{2,10},{3,251},{4,12},{5,253},{6,14},{7,255},{8,16},... | collective-permute-start | bytes 688136 | tf_op jit(solution)/shard_map/ppermute | solution.py:393
  194.2 23.9 %collective-permute-start.26 = (bf16[58,16,128]{2,1,0:T(8,128)(2,1)}, bf16[58,16,128]{2,1,0:T(8,128)(2,1)S(1)}, u32[]{:S(2)}, u32[]{:S(2)}) collective-permute-start(bf16[58,16,128]{2,1,0:T(8,128)(2,1)} %get-tuple-element.115), channel_id=1, source_target_pairs={{0,8},{1,249},{2,10},{3,251},{4,12},{5,253},{6,14},{7,255},{8,16},... | collective-permute-start | bytes 712712 | tf_op jit(solution)/shard_map/ppermute | solution.py:393
  203.4 44.7 %all-to-all-start.2 = ((bf16[8,16,16,128]{3,2,1,0:T(8,128)(2,1)}), bf16[8,16,16,128]{3,2,1,0:T(8,128)(2,1)S(1)}, u32[]{:S(2)}, u32[]{:S(2)}) async-start(bf16[8,16,16,128]{3,2,1,0:T(8,128)(2,1)} %get-tuple-element.126), calls=%async_computation.2 | async-start | bytes 1048576 | tf_op jit(solution)/shard_map/all_to_all | solution.py:513
  216.1 11.9 %collective-permute-start.27 = (bf16[40,16,128]{2,1,0:T(8,128)(2,1)}, bf16[40,16,128]{2,1,0:T(8,128)(2,1)}, u32[]{:S(2)}, u32[]{:S(2)}) collective-permute-start(bf16[40,16,128]{2,1,0:T(8,128)(2,1)} %slice.36), channel_id=1, source_target_pairs={{0,8},{1,249},{2,10},{3,251},{4,12},{5,253},{6,14},{7,255},{8,16},... | collective-permute-start | bytes 491528 | tf_op jit(solution)/shard_map/ppermute | solution.py:393
  218.8 12.2 %collective-permute-start.28 = (bf16[42,16,128]{2,1,0:T(8,128)(2,1)}, bf16[42,16,128]{2,1,0:T(8,128)(2,1)S(1)}, u32[]{:S(2)}, u32[]{:S(2)}) collective-permute-start(bf16[42,16,128]{2,1,0:T(8,128)(2,1)} %get-tuple-element.119), channel_id=1, source_target_pairs={{0,8},{1,249},{2,10},{3,251},{4,12},{5,253},{6,14},{7,255},{8,16},... | collective-permute-start | bytes 516104 | tf_op jit(solution)/shard_map/ppermute | solution.py:393
  248.1 15.8 %all-to-all-start = ((bf16[8,18,16,128]{3,2,1,0:T(8,128)(2,1)}), bf16[8,18,16,128]{3,2,1,0:T(8,128)(2,1)S(1)}, u32[]{:S(2)}, u32[]{:S(2)}) async-start(bf16[8,18,16,128]{3,2,1,0:T(8,128)(2,1)} %shard_map.137), calls=%async_computation | async-start | bytes 1179648 | tf_op jit(solution)/shard_map/all_to_all | solution.py:554
  (42 other events, 300.2 us)

commit v2 on v1

--- a/solution.py
+++ b/solution.py
@@ -14,10 +14,9 @@
 PENALTY = 1e30
 SMEM = pltpu.SMEM
 VMEM = pltpu.VMEM
-GROUPS = (8,)
-
-
-def call(body, outs, ins, specs=None, scratch=(), mebibytes=2, aliases=None, outside=()):
+
+
+def call(body, outs, ins, specs=None, scratch=(), mebibytes=2, aliases=None, outside=(), plain=()):
     specs = specs or [vm() for _ in ins]
     single = not isinstance(outs, (list, tuple))
     out_list = [outs] if single else list(outs)
@@ -28,7 +27,7 @@
     gridded = any(spec.block_shape is not None for spec in specs)
     result = pl.pallas_call(
         body,
-        out_shape=[x if INTERPRET or i in outside else VMEM(x.shape, x.dtype) for i, x in enumerate(out_list)],
+        out_shape=[x if INTERPRET or i in outside or i in plain else VMEM(x.shape, x.dtype) for i, x in enumerate(out_list)],
         in_specs=specs,
         out_specs=[pl.BlockSpec(memory_space=pl.ANY) if i in outside else vm() for i in range(len(out_list))],
         **({"grid": (1,)} if gridded else {}),
@@ -46,6 +45,10 @@
 
 def sm():
     return pl.BlockSpec(memory_space=SMEM)
+
+
+def outside_vmem(arrays):
+    return arrays if INTERPRET else [pltpu.with_memory_space_constraint(x, pltpu.HBM) for x in arrays]
 
 
 def struct(shape, dtype=BF16):
@@ -119,9 +122,31 @@
         norm_ref[j : j + 1, :] = jnp.sum(acc * values, axis=0, keepdims=True)
 
 
-def cross_kernel(count, k, turn, words, chosen, info, lists, table_ref, rows_ref, *refs):
+def pick_images(distance, step, info, taken, blocks, group_ref, picked, stored):
+    core = info[0]
+    paired = len(blocks) - 1
+    for s in range(picked.shape[0]):
+        for c in range(2):
+            slot = taken[distance * 2 * picked.shape[0] + 2 * s + c]
+            if paired:
+                picked[s, 2 * c + core] = blocks[0][slot]
+                picked[s, 2 * c + 1 - core] = blocks[1][slot]
+            else:
+                picked[s, c] = blocks[0][slot]
+    tiles = 2 + 2 * paired
+    store = pltpu.make_async_copy(picked.at[:, 0:tiles], group_ref.at[:, step : step + tiles], stored)
+    store.start()
+    return store
+
+
+def pick_kernel(distance, step, info, taken, block_a, block_b, group_in, group_ref, picked, stored):
+    del group_in
+    pick_images(distance, step, info, taken, (block_a, block_b), group_ref, picked, stored).wait()
+
+
+def cross_kernel(count, k, turn, words, chosen, deps, info, lists, table_ref, rows_ref, *refs):
     idx, arrived, picked, stored = refs[-4:]
-    refs = refs[:-4]
+    refs = refs[deps:-4]
     fetch = pltpu.make_async_copy(lists.at[k - 1], idx, arrived)
     fetch.start()
     if chosen is None:
@@ -131,18 +156,7 @@
         taken, refs = refs[0], refs[1:]
         blocks, refs = refs[: 1 + paired], refs[1 + paired + (not fresh) :]
         out_ref, group_ref, turned, gathered, products = refs
-        core = info[0]
-        for s in range(picked.shape[0]):
-            for c in range(2):
-                slot = taken[distance * 2 * picked.shape[0] + 2 * s + c]
-                if paired:
-                    picked[s, 2 * c + core] = blocks[0][slot]
-                    picked[s, 2 * c + 1 - core] = blocks[1][slot]
-                else:
-                    picked[s, c] = blocks[0][slot]
-        tiles = 2 + 2 * paired
-        store = pltpu.make_async_copy(picked.at[:, 0:tiles], group_ref.at[:, step : step + tiles], stored)
-        store.start()
+        store = pick_images(distance, step, info, taken, blocks, group_ref, picked, stored)
     padded = gathered.shape[1]
     total = turned.shape[2]
     half = total // 2
@@ -308,8 +322,16 @@
 
 
 def match_kernel(plan, width, topk, padded, pairs, info, *refs):
-    group, pen, live, near_row, near_lane, own_row, own_lane = refs[:7]
-    nearest, margin, similarity, lhs, rhs, squares, least, less, query = refs[10:]
+    group, pen, live, near_row, near_lane, own_row, own_lane, lhs_in, rhs_in, squares_in = refs[:10]
+    nearest, margin, similarity, lhs, rhs, squares, least, less, query, left, right = refs[10:]
+    ready = lhs_in.shape[0]
+    bring = (
+        pltpu.make_async_copy(lhs_in, lhs.at[0:ready], left),
+        pltpu.make_async_copy(rhs_in, rhs.at[0:ready], right),
+    )
+    for copy in bring:
+        copy.start()
+    squares[0:ready] = squares_in[...]
     pair_total = nearest.shape[0]
     subs = group.shape[0]
     end = group.shape[1]
@@ -332,6 +354,9 @@
         line, lane = divmod(r * padded, LANES)
         both = jnp.concatenate((cosine[line : line + 1], cosine[line + 1 : line + 2]), axis=1) if line < 3 else cosine[3:4]
         similarity[r : r + 1, :] = both[:, lane : lane + topk]
+
+    for copy in bring:
+        copy.wait()
 
     def pair(p, carry):
         asked = pairs[2 * p]
@@ -417,9 +442,10 @@
     taken_here = lax.dynamic_index_in_dim(send_table, w, 1, keepdims=False).reshape(words, targets)
     taken_mine = taken_here[lax.rem(w + jnp.where(core == 0, words - away, away), words)].reshape(-1)
 
-    def cross(k, distance=None, sources=(), group=None, step=0, tiles=0):
-        specs = [sm(), pl.BlockSpec(memory_space=pl.ANY), vm(), vm()]
-        ins = [info, near_order, table3, table]
+    def cross(k, deps=(), distance=None, sources=(), group=None, step=0, tiles=0):
+        apart = pl.BlockSpec(memory_space=pl.ANY)
+        specs = [sm(), apart, vm(), vm()] + [apart] * len(deps)
+        ins = [info, near_order, table3, table, *deps]
         outs = [struct((2, 4, LANES), F32)]
         chosen, aliases = None, {}
         if sources:
@@ -431,9 +457,9 @@
             if group is not None:
                 aliases = {len(ins): 1}
                 ins += [group]
-                specs += [pl.BlockSpec(memory_space=pl.ANY)]
+                specs += [apart]
         result = call(
-            functools.partial(cross_kernel, topk, k, (reach + 1 - k, reach + k), words, chosen),
+            functools.partial(cross_kernel, topk, k, (reach + 1 - k, reach + k), words, chosen, len(deps)),
             outs,
             ins,
             specs,
@@ -491,28 +517,32 @@
     b = send(call(first_kernel, struct((held + 2, depth, points)), first))
     norm = jnp.where(core == 0, norm, 0.0)
     full = reach - 4
-    cut = GROUPS[0]
     blocks = [(descriptors,), (a, b)]
     group = None
-    exchange = []
-    plan = [(0, 1, 2 * cut, 2, 0), (0, 0, 1, 0, 4 * cut), (1, 2 * cut + 1, 2 * (full - cut), 2, 0)]
+    tiles = 4 * full + 2
+    plan = [(0, 1, 2 * full, 2, 0), (0, 0, 1, 0, 4 * full)]
+    deps = {4: (trims,), 5: (flat_pairs,), 6: (pen,), 7: (live,), 8: (near_row, near_lane), 9: (own_row, own_lane)}
+    late = {k: cross(k) for k in range(full + 1, reach + 1)}
 
     def step(k):
         nonlocal group
         d = k - 2
-        if d > full:
-            return cross(k)
-        if d == 0:
-            where, tiles = 4 * cut, 4 * cut + 2
-        elif d <= cut:
-            where, tiles = 4 * (d - 1), 4 * cut + 2
-        else:
-            where, tiles = 4 * (d - 1 - cut), 4 * (full - cut)
-        product, group = cross(k, d, blocks[d], group, where, tiles)
-        if d in (cut, full):
-            exchange.append(lax.all_to_all(group, "sub", 0, 0, tiled=True))
-            group = None
-        return product
+        if k <= full:
+            where = 4 * (d - 1) if d else 4 * full
+            product, group = cross(k, deps.get(k, ()), d, blocks[d], group, where, tiles)
+            return product
+        if d <= full:
+            group = call(
+                functools.partial(pick_kernel, d, 4 * (d - 1)),
+                struct((subs, tiles, depth, points)),
+                (info, taken_mine, *blocks[d], group),
+                [sm(), sm(), vm(), vm(), pl.BlockSpec(memory_space=pl.ANY)],
+                (pltpu.VMEM((subs, 4, depth, points), BF16), pltpu.SemaphoreType.DMA(())),
+                2,
+                {4: 0},
+                {0},
+            )
+        return late[k]
 
     for k in range(2, full + 1):
         product = step(k)
@@ -534,6 +564,8 @@
     for k in range(full + 2, reach + 1):
         size -= targets
         product = step(k)
+        if k == full + 2:
+            exchange = [lax.all_to_all(group, "sub", 0, 0, tiled=True)]
         if k == reach:
             kept = call(keep_kernel, struct((2, 4, LANES), F32), (b, product))
         a = send(a[targets:])
@@ -554,32 +586,42 @@
     tail = lax.all_to_all(tail, "sub", 0, 0, tiled=True)
 
     total = 2 * words
+    early = 2 * (2 * full + 1)
     held_struct = (
-        struct((total, points, width + depth)),
-        struct((total, width + depth, points)),
-        struct((total, points), F32),
+        struct((early, points, width + depth)),
+        struct((early, width + depth, points)),
+        struct((early, points), F32),
     )
     ready = call(
         functools.partial(early_kernel, len(exchange), plan),
         held_struct,
         (info, *exchange, pen),
         [sm()] + [vm()] * (len(exchange) + 1),
+        (),
+        12,
+        None,
+        (),
+        {0, 1},
     )
     plan = [(0, 2 * full + 1, 2 * (steps - 1), 2, 0), (0, 2 * reach - 1, 1, 1, 4 * (steps - 1))]
-    ins = (flat_pairs, info, tail, pen, live, near_row, near_lane, own_row, own_lane, *ready)
+    ins = (flat_pairs, info, tail, pen, live, near_row, near_lane, own_row, own_lane, *outside_vmem(ready[:2]), ready[2])
     rows = struct((pair_total, points), F32)
-    nearest, margin, similarity, *_ = call(
+    nearest, margin, similarity = call(
         functools.partial(match_kernel, plan, width, topk, padded),
-        (rows, rows, struct((per, topk), F32), *held_struct),
+        (rows, rows, struct((per, topk), F32)),
         ins,
-        [sm(), sm()] + [vm()] * (len(ins) - 2),
+        [sm(), sm()] + [vm()] * (len(ins) - 5) + [pl.BlockSpec(memory_space=pl.ANY)] * 2 + [vm()],
         (
+            pltpu.VMEM((total, points, width + depth), BF16),
+            pltpu.VMEM((total, width + depth, points), BF16),
+            pltpu.VMEM((total, points), F32),
             pltpu.VMEM((pair_total, 8, points), F32),
             pltpu.VMEM((pair_total, 8, points), F32),
             pltpu.VMEM((pair_total, points), F32),
+            pltpu.SemaphoreType.DMA(()),
+            pltpu.SemaphoreType.DMA(()),
         ),
-        4,
-        {9: 3, 10: 4, 11: 5},
+        10,
     )
     return similarity, nearest[None, None], margin[None, None]
 

time: 277 us -> 246 us (0.89)
  local copies, waits for them, and re-layouts: 30.2 us -> 12.6 us
  starting transfers between devices: 134 us -> 121 us
  waiting for transfers between devices: 32.7 us -> 40.5 us
  other arithmetic: 6.45 us -> 0.54 us
    all_to_all x2 -> x1, starting transfers between devices: 15.8 us -> 4.67 us  [local(): exchange = [lax.all_to_all(group, 'sub', 0, 0, tiled=True)]]
    unnamed x66 -> x48, local copies, waits for them, and re-layouts: 15.7 us -> 6.39 us
    ppermute x32, waiting for transfers between devices: 32.7 us -> 40.5 us  [send(): return lax.ppermute(x, ('word', 'sub'), pairs_of_ring)]
    pallas_call x37 -> x39, Pallas kernels: 68.8 us -> 67.2 us  [call(): pl.pallas_call(body, out_shape=[x if INTERPRET or i in outside or i in pl...]
  transfers between devices with their start and end apart: 36 -> 35, of which waited for: 20 -> 28; matrix products, arithmetic and copies ran while one was open for 9% -> 3% of each run, Pallas kernels for 23% -> 25%
where the time goes in v2:
time: 246 us; the launch traced here: 244 us
  starting transfers between devices  121 us (49%)
  Pallas kernels  67.2 us (27%)
  waiting for transfers between devices  40.5 us (16%)
  local copies, waits for them, and re-layouts  12.6 us (5%)
    ppermute x32, starting transfers between devices, send(): return lax.ppermute(x, ('word', 'sub'), pairs_of_ring)  69.5 us
    pallas_call x39, Pallas kernels, call(): pl.pallas_call(body, out_shape=[x if INTERPRET or i in outside or i in pl...  67.2 us
    ppermute x1, starting transfers between devices, local(): lax.ppermute(descriptors, 'sub', [(j, j ^ 1) for j in range(subs)])  42.2 us
    ppermute x32, waiting for transfers between devices, send(): return lax.ppermute(x, ('word', 'sub'), pairs_of_ring)  40.5 us
    unnamed x48, local copies, waits for them, and re-layouts  6.39 us
    all_to_all x1, starting transfers between devices, local(): tail = lax.all_to_all(tail, 'sub', 0, 0, tiled=True)  4.96 us
  transfers between devices with their start and end apart: 35, of which 28 were waited for; matrix products, arithmetic and copies ran while one was open for 3% of the time, Pallas kernels for 25%

profile of v2, /device:TPU:38, one launch (start us, length us, event | category | flops | bytes accessed | tf_op | source)
XLA Modules:
  0.0 243.8 jit_solution(8805030240079529675)
XLA Ops:
  0.7 4.8 %collective-permute-start = (bf16[64,16,128]{2,1,0:T(8,128)(2,1)}, bf16[64,16,128]{2,1,0:T(8,128)(2,1)S(1)}, u32[]{:S(2)}, u32[]{:S(2)}) collective-permute-start(bf16[64,16,128]{2,1,0:T(8,128)(2,1)} %refs_1_.1), channel_id=1, source_target_pairs={{0,8},{1,249},{2,10},{3,251},{4,12},{5,253},{6,14},{7,255},{8,16},... | collective-permute-start | bytes 786440 | tf_op jit(solution)/shard_map/ppermute | solution.py:418
  5.5 42.2 %collective-permute-start.12 = (bf16[64,16,128]{2,1,0:T(8,128)(2,1)}, bf16[64,16,128]{2,1,0:T(8,128)(2,1)S(1)}, u32[]{:S(2)}, u32[]{:S(2)}) collective-permute-start(bf16[64,16,128]{2,1,0:T(8,128)(2,1)} %refs_1_.1), channel_id=1, source_target_pairs={{0,1},{1,0},{2,3},{3,2},{4,5},{5,4},{6,7},{7,6},{8,9},{9,8},{10,11... | collective-permute-start | bytes 786440 | tf_op jit(solution)/shard_map/ppermute | solution.py:421
  52.5 2.9 %shard_map.104.cross_ref = f32[2,4,128]{2,1,0:T(4,128)S(1)} custom-call(s32[4]{0:T(128)S(1)} %pad_add_fusion.info, s32[16,1,800]{2,1,0:T(1,128)S(1)} %reshape.226.lists, f32[2048,1,128]{2,1,0:T(1,128)S(1)} %bitcast.89, f32[2048,128]{1,0:T(8,128)S(1)} %get-tuple-element.65.rows_ref), custom_call_target="tpu_custom_call" | custom-call | tf_op jit(solution)/shard_map/pallas_call | solution.py:28
  58.1 3.1 %shard_map.106 = (f32[2,4,128]{2,1,0:T(4,128)S(1)}, bf16[8,50,16,128]{3,2,1,0:T(8,128)(2,1)}) custom-call(s32[4]{0:T(128)S(1)} %pad_add_fusion.info, s32[16,1,800]{2,1,0:T(1,128)S(1)} %reshape.226.lists, f32[2048,1,128]{2,1,0:T(1,128)S(1)} %bitcast.90, f32[2048,128]{1,0:T(8,128)S(1)} %get-tuple-element.65.rows_ref, ...), custom_call_target="tpu_custom_call" | custom-call | tf_op jit(solution)/shard_map/pallas_call | solution.py:28
  61.3 3.8 %collective-permute-done.13.recv.refs_2_ = bf16[66,16,128]{2,1,0:T(8,128)(2,1)S(1)} collective-permute-done((bf16[66,16,128]{2,1,0:T(8,128)(2,1)S(1)}, bf16[66,16,128]{2,1,0:T(8,128)(2,1)S(1)}, u32[]{:S(2)}, u32[]{:S(2)}) %collective-permute-start.13) | collective-permute-done | bytes 270368 | tf_op jit(solution)/shard_map/ppermute | solution.py:418
  69.8 3.1 %shard_map.108 = (f32[2,4,128]{2,1,0:T(4,128)S(1)}, bf16[8,50,16,128]{3,2,1,0:T(8,128)(2,1)}) custom-call(s32[4]{0:T(128)S(1)} %pad_add_fusion.info, s32[16,1,800]{2,1,0:T(1,128)S(1)} %reshape.226.lists, f32[2048,1,128]{2,1,0:T(1,128)S(1)} %bitcast.91, f32[2048,128]{1,0:T(8,128)S(1)} %get-tuple-element.65.rows_ref, ...), custom_call_target="tpu_custom_call", output_to_operand_aliasing={{1}: (7, {})} | custom-call | tf_op jit(solution)/shard_map/pallas_call | solution.py:28
  80.3 3.1 %shard_map.110 = (f32[2,4,128]{2,1,0:T(4,128)S(1)}, bf16[8,50,16,128]{3,2,1,0:T(8,128)(2,1)}) custom-call(s32[4]{0:T(128)S(1)} %pad_add_fusion.info, s32[16,1,800]{2,1,0:T(1,128)S(1)} %reshape.226.lists, f32[2048,1,128]{2,1,0:T(1,128)S(1)} %bitcast.92, f32[2048,128]{1,0:T(8,128)S(1)} %get-tuple-element.65.rows_ref, ...), custom_call_target="tpu_custom_call", output_to_operand_aliasing={{1}: (8, {})} | custom-call | tf_op jit(solution)/shard_map/pallas_call | solution.py:28
  89.2 3.1 %shard_map.112 = (f32[2,4,128]{2,1,0:T(4,128)S(1)}, bf16[8,50,16,128]{3,2,1,0:T(8,128)(2,1)}) custom-call(s32[4]{0:T(128)S(1)} %pad_add_fusion.info, s32[16,1,800]{2,1,0:T(1,128)S(1)} %reshape.226.lists, f32[2048,1,128]{2,1,0:T(1,128)S(1)} %bitcast.93, f32[2048,128]{1,0:T(8,128)S(1)} %get-tuple-element.65.rows_ref, ...), custom_call_target="tpu_custom_call", output_to_operand_aliasing={{1}: (8, {})} | custom-call | tf_op jit(solution)/shard_map/pallas_call | solution.py:28
  98.8 3.1 %shard_map.114 = (f32[2,4,128]{2,1,0:T(4,128)S(1)}, bf16[8,50,16,128]{3,2,1,0:T(8,128)(2,1)}) custom-call(s32[4]{0:T(128)S(1)} %pad_add_fusion.info, s32[16,1,800]{2,1,0:T(1,128)S(1)} %reshape.226.lists, f32[2048,1,128]{2,1,0:T(1,128)S(1)} %bitcast.94, f32[2048,128]{1,0:T(8,128)S(1)} %get-tuple-element.65.rows_ref, ...), custom_call_target="tpu_custom_call", output_to_operand_aliasing={{1}: (8, {})} | custom-call | tf_op jit(solution)/shard_map/pallas_call | solution.py:28
  108.5 3.1 %shard_map.116 = (f32[2,4,128]{2,1,0:T(4,128)S(1)}, bf16[8,50,16,128]{3,2,1,0:T(8,128)(2,1)}) custom-call(s32[4]{0:T(128)S(1)} %pad_add_fusion.info, s32[16,1,800]{2,1,0:T(1,128)S(1)} %reshape.226.lists, f32[2048,1,128]{2,1,0:T(1,128)S(1)} %bitcast.95, f32[2048,128]{1,0:T(8,128)S(1)} %get-tuple-element.65.rows_ref, ...), custom_call_target="tpu_custom_call", output_to_operand_aliasing={{1}: (8, {})} | custom-call | tf_op jit(solution)/shard_map/pallas_call | solution.py:28
  119.0 3.1 %shard_map.118 = (f32[2,4,128]{2,1,0:T(4,128)S(1)}, bf16[8,50,16,128]{3,2,1,0:T(8,128)(2,1)}) custom-call(s32[4]{0:T(128)S(1)} %pad_add_fusion.info, s32[16,1,800]{2,1,0:T(1,128)S(1)} %reshape.226.lists, f32[2048,1,128]{2,1,0:T(1,128)S(1)} %bitcast.96, f32[2048,128]{1,0:T(8,128)S(1)} %get-tuple-element.65.rows_ref, ...), custom_call_target="tpu_custom_call", output_to_operand_aliasing={{1}: (9, {})} | custom-call | tf_op jit(solution)/shard_map/pallas_call | solution.py:28
  127.8 3.1 %shard_map.120 = (f32[2,4,128]{2,1,0:T(4,128)S(1)}, bf16[8,50,16,128]{3,2,1,0:T(8,128)(2,1)}) custom-call(s32[4]{0:T(128)S(1)} %pad_add_fusion.info, s32[16,1,800]{2,1,0:T(1,128)S(1)} %reshape.226.lists, f32[2048,1,128]{2,1,0:T(1,128)S(1)} %bitcast.97, f32[2048,128]{1,0:T(8,128)S(1)} %get-tuple-element.65.rows_ref, ...), custom_call_target="tpu_custom_call", output_to_operand_aliasing={{1}: (9, {})} | custom-call | tf_op jit(solution)/shard_map/pallas_call | solution.py:28
  137.3 3.1 %shard_map.122 = (f32[2,4,128]{2,1,0:T(4,128)S(1)}, bf16[8,50,16,128]{3,2,1,0:T(8,128)(2,1)}) custom-call(s32[4]{0:T(128)S(1)} %pad_add_fusion.info, s32[16,1,800]{2,1,0:T(1,128)S(1)} %reshape.226.lists, f32[2048,1,128]{2,1,0:T(1,128)S(1)} %bitcast.98, f32[2048,128]{1,0:T(8,128)S(1)} %get-tuple-element.65.rows_ref, ...), custom_call_target="tpu_custom_call", output_to_operand_aliasing={{1}: (7, {})} | custom-call | tf_op jit(solution)/shard_map/pallas_call | solution.py:28
  146.9 3.1 %shard_map.124 = (f32[2,4,128]{2,1,0:T(4,128)S(1)}, bf16[8,50,16,128]{3,2,1,0:T(8,128)(2,1)}) custom-call(s32[4]{0:T(128)S(1)} %pad_add_fusion.info, s32[16,1,800]{2,1,0:T(1,128)S(1)} %reshape.226.lists, f32[2048,1,128]{2,1,0:T(1,128)S(1)} %bitcast.99, f32[2048,128]{1,0:T(8,128)S(1)} %get-tuple-element.65.rows_ref, ...), custom_call_target="tpu_custom_call", output_to_operand_aliasing={{1}: (7, {})} | custom-call | tf_op jit(solution)/shard_map/pallas_call | solution.py:28
  156.5 3.1 %shard_map.126 = (f32[2,4,128]{2,1,0:T(4,128)S(1)}, bf16[8,50,16,128]{3,2,1,0:T(8,128)(2,1)}) custom-call(s32[4]{0:T(128)S(1)} %pad_add_fusion.info, s32[16,1,800]{2,1,0:T(1,128)S(1)} %reshape.226.lists, f32[2048,1,128]{2,1,0:T(1,128)S(1)} %bitcast.100, f32[2048,128]{1,0:T(8,128)S(1)} %get-tuple-element.65.rows_ref, ...), custom_call_target="tpu_custom_call", output_to_operand_aliasing={{1}: (7, {})} | custom-call | tf_op jit(solution)/shard_map/pallas_call | solution.py:28
  167.4 6.4 %collective-permute-done.11.recv_a.block_a = bf16[64,16,128]{2,1,0:T(8,128)(2,1)S(1)} collective-permute-done((bf16[64,16,128]{2,1,0:T(8,128)(2,1)S(1)}, bf16[64,16,128]{2,1,0:T(8,128)(2,1)S(1)}, u32[]{:S(2)}, u32[]{:S(2)}) %collective-permute-start.11) | collective-permute-done | bytes 262176 | tf_op jit(solution)/shard_map/ppermute | solution.py:418
  175.1 4.7 %all-to-all-start.1 = ((bf16[8,50,16,128]{3,2,1,0:T(8,128)(2,1)}), bf16[8,50,16,128]{3,2,1,0:T(8,128)(2,1)S(1)}, u32[]{:S(2)}, u32[]{:S(2)}) async-start(bf16[8,50,16,128]{3,2,1,0:T(8,128)(2,1)} %shard_map.139), calls=%async_computation.1 | async-start | bytes 3276800 | tf_op jit(solution)/shard_map/all_to_all | solution.py:568
  187.3 2.9 %shard_map.130.cross_ref = f32[2,4,128]{2,1,0:T(4,128)S(1)} custom-call(s32[4]{0:T(128)S(1)} %pad_add_fusion.info, s32[16,1,800]{2,1,0:T(1,128)S(1)} %reshape.226.lists, f32[2048,1,128]{2,1,0:T(1,128)S(1)} %bitcast.102, f32[2048,128]{1,0:T(8,128)S(1)} %get-tuple-element.65.rows_ref), custom_call_target="tpu_custom_call" | custom-call | tf_op jit(solution)/shard_map/pallas_call | solution.py:28
  209.1 4.0 %collective-permute-start.32 = (bf16[10,16,128]{2,1,0:T(8,128)(2,1)S(1)}, bf16[10,16,128]{2,1,0:T(8,128)(2,1)S(1)}, u32[]{:S(2)}, u32[]{:S(2)}) collective-permute-start(bf16[10,16,128]{2,1,0:T(8,128)(2,1)S(1)} %get-tuple-element.116), channel_id=1, source_target_pairs={{0,8},{1,249},{2,10},{3,251},{4,12},{5,253},{6,14},{7,255},{8,16},... | collective-permute-start | bytes 122888 | tf_op jit(solution)/shard_map/ppermute | solution.py:418
  213.0 4.1 %collective-permute-start.31 = (bf16[8,16,128]{2,1,0:T(8,128)(2,1)S(1)}, bf16[8,16,128]{2,1,0:T(8,128)(2,1)S(1)}, u32[]{:S(2)}, u32[]{:S(2)}) collective-permute-start(bf16[8,16,128]{2,1,0:T(8,128)(2,1)S(1)} %slice.38), channel_id=1, source_target_pairs={{0,8},{1,249},{2,10},{3,251},{4,12},{5,253},{6,14},{7,255},{8,16},... | collective-permute-start | bytes 98312 | tf_op jit(solution)/shard_map/ppermute | solution.py:418
  217.2 2.9 %collective-permute-done.31.refs_6_ = bf16[8,16,128]{2,1,0:T(8,128)(2,1)S(1)} collective-permute-done((bf16[8,16,128]{2,1,0:T(8,128)(2,1)S(1)}, bf16[8,16,128]{2,1,0:T(8,128)(2,1)S(1)}, u32[]{:S(2)}, u32[]{:S(2)}) %collective-permute-start.31) | collective-permute-done | bytes 32800 | tf_op jit(solution)/shard_map/ppermute | solution.py:418
  221.5 5.0 %all-to-all-start = ((bf16[8,18,16,128]{3,2,1,0:T(8,128)(2,1)}), bf16[8,18,16,128]{3,2,1,0:T(8,128)(2,1)S(1)}, u32[]{:S(2)}, u32[]{:S(2)}) async-start(bf16[8,18,16,128]{3,2,1,0:T(8,128)(2,1)} %shard_map.137), calls=%async_computation | async-start | bytes 1179648 | tf_op jit(solution)/shard_map/all_to_all | solution.py:586
  226.5 7.4 %shard_map.140 = (bf16[50,128,144]{2,1,0:T(8,128)(2,1)S(1)}, bf16[50,144,128]{2,1,0:T(8,128)(2,1)S(1)}, f32[50,128]{1,0:T(8,128)S(1)}) custom-call(s32[4]{0:T(128)S(1)} %pad_add_fusion.info, bf16[8,50,16,128]{3,2,1,0:T(8,128)(2,1)S(1)} %all-to-all-done.1.refs_0_, f32[64,128]{1,0:T(8,128)S(1)} %copy-done.4), custom_call_target="tpu_custom_call" | custom-call | tf_op jit(solution)/shard_map/pallas_call | solution.py:28
  236.9 5.0 %shard_map.141 = (f32[32,128]{1,0:T(8,128)S(1)}, f32[32,128]{1,0:T(8,128)S(1)}, f32[8,50]{1,0:T(8,128)S(1)}) custom-call(s32[64]{0:T(128)S(1)} %copy-done.15, s32[4]{0:T(128)S(1)} %pad_add_fusion.info, bf16[8,18,16,128]{3,2,1,0:T(8,128)(2,1)S(1)} %all-to-all-done.refs_0_, f32[64,128]{1,0:T(8,128)S(1)} %copy-done.4, f32[32,128]{1,0:T(8,128)S(1)} %copy-done.9, ...), custom_call_target="tpu_custom_call" | custom-call | tf_op jit(solution)/shard_map/pallas_call | solution.py:28
  (184 shorter events, 111.7 us)
Async XLA Ops:
  0.7 66.5 %collective-permute-start = (bf16[64,16,128]{2,1,0:T(8,128)(2,1)}, bf16[64,16,128]{2,1,0:T(8,128)(2,1)S(1)}, u32[]{:S(2)}, u32[]{:S(2)}) collective-permute-start(bf16[64,16,128]{2,1,0:T(8,128)(2,1)} %refs_1_.1), channel_id=1, source_target_pairs={{0,8},{1,249},{2,10},{3,251},{4,12},{5,253},{6,14},{7,255},{8,16},... | collective-permute-start | bytes 786440 | tf_op jit(solution)/shard_map/ppermute | solution.py:418
  5.5 49.9 %collective-permute-start.12 = (bf16[64,16,128]{2,1,0:T(8,128)(2,1)}, bf16[64,16,128]{2,1,0:T(8,128)(2,1)S(1)}, u32[]{:S(2)}, u32[]{:S(2)}) collective-permute-start(bf16[64,16,128]{2,1,0:T(8,128)(2,1)} %refs_1_.1), channel_id=1, source_target_pairs={{0,1},{1,0},{2,3},{3,2},{4,5},{5,4},{6,7},{7,6},{8,9},{9,8},{10,11... | collective-permute-start | bytes 786440 | tf_op jit(solution)/shard_map/ppermute | solution.py:421
  55.5 9.6 %collective-permute-start.13 = (bf16[66,16,128]{2,1,0:T(8,128)(2,1)S(1)}, bf16[66,16,128]{2,1,0:T(8,128)(2,1)S(1)}, u32[]{:S(2)}, u32[]{:S(2)}) collective-permute-start(bf16[66,16,128]{2,1,0:T(8,128)(2,1)S(1)} %shard_map.105), channel_id=1, source_target_pairs={{0,8},{1,249},{2,10},{3,251},{4,12},{5,253},{6,14},{7,255},{8,16},... | collective-permute-start | bytes 811016 | tf_op jit(solution)/shard_map/ppermute | solution.py:418
  65.1 9.6 %collective-permute-start.14 = (bf16[66,16,128]{2,1,0:T(8,128)(2,1)S(1)}, bf16[66,16,128]{2,1,0:T(8,128)(2,1)S(1)}, u32[]{:S(2)}, u32[]{:S(2)}) collective-permute-start(bf16[66,16,128]{2,1,0:T(8,128)(2,1)S(1)} %get-tuple-element.67), channel_id=1, source_target_pairs={{0,8},{1,249},{2,10},{3,251},{4,12},{5,253},{6,14},{7,255},{8,16},... | collective-permute-start | bytes 811016 | tf_op jit(solution)/shard_map/ppermute | solution.py:418
  67.2 10.4 %collective-permute-start.1 = (bf16[64,16,128]{2,1,0:T(8,128)(2,1)S(1)}, bf16[64,16,128]{2,1,0:T(8,128)(2,1)S(1)}, u32[]{:S(2)}, u32[]{:S(2)}) collective-permute-start(bf16[64,16,128]{2,1,0:T(8,128)(2,1)S(1)} %collective-permute-done.refs_1_), channel_id=1, source_target_pairs={{0,8},{1,249},{2,10},{3,251},{4,12},{5,253},{6,14},{7,255},{8,16},... | collective-permute-start | bytes 786440 | tf_op jit(solution)/shard_map/ppermute | solution.py:418
  74.8 9.6 %collective-permute-start.15 = (bf16[66,16,128]{2,1,0:T(8,128)(2,1)S(1)}, bf16[66,16,128]{2,1,0:T(8,128)(2,1)S(1)}, u32[]{:S(2)}, u32[]{:S(2)}) collective-permute-start(bf16[66,16,128]{2,1,0:T(8,128)(2,1)S(1)} %get-tuple-element.71), channel_id=1, source_target_pairs={{0,8},{1,249},{2,10},{3,251},{4,12},{5,253},{6,14},{7,255},{8,16},... | collective-permute-start | bytes 811016 | tf_op jit(solution)/shard_map/ppermute | solution.py:418
  77.5 9.6 %collective-permute-start.2 = (bf16[64,16,128]{2,1,0:T(8,128)(2,1)S(1)}, bf16[64,16,128]{2,1,0:T(8,128)(2,1)S(1)}, u32[]{:S(2)}, u32[]{:S(2)}) collective-permute-start(bf16[64,16,128]{2,1,0:T(8,128)(2,1)S(1)} %collective-permute-done.1.refs_2_), channel_id=1, source_target_pairs={{0,8},{1,249},{2,10},{3,251},{4,12},{5,253},{6,14},{7,255},{8,16},... | collective-permute-start | bytes 786440 | tf_op jit(solution)/shard_map/ppermute | solution.py:418
  84.4 9.6 %collective-permute-start.16 = (bf16[66,16,128]{2,1,0:T(8,128)(2,1)S(1)}, bf16[66,16,128]{2,1,0:T(8,128)(2,1)S(1)}, u32[]{:S(2)}, u32[]{:S(2)}) collective-permute-start(bf16[66,16,128]{2,1,0:T(8,128)(2,1)S(1)} %get-tuple-element.75), channel_id=1, source_target_pairs={{0,8},{1,249},{2,10},{3,251},{4,12},{5,253},{6,14},{7,255},{8,16},... | collective-permute-start | bytes 811016 | tf_op jit(solution)/shard_map/ppermute | solution.py:418
  87.2 9.6 %collective-permute-start.3 = (bf16[64,16,128]{2,1,0:T(8,128)(2,1)S(1)}, bf16[64,16,128]{2,1,0:T(8,128)(2,1)S(1)}, u32[]{:S(2)}, u32[]{:S(2)}) collective-permute-start(bf16[64,16,128]{2,1,0:T(8,128)(2,1)S(1)} %collective-permute-done.2.refs_2_), channel_id=1, source_target_pairs={{0,8},{1,249},{2,10},{3,251},{4,12},{5,253},{6,14},{7,255},{8,16},... | collective-permute-start | bytes 786440 | tf_op jit(solution)/shard_map/ppermute | solution.py:418
  96.8 9.6 %collective-permute-start.4 = (bf16[64,16,128]{2,1,0:T(8,128)(2,1)S(1)}, bf16[64,16,128]{2,1,0:T(8,128)(2,1)S(1)}, u32[]{:S(2)}, u32[]{:S(2)}) collective-permute-start(bf16[64,16,128]{2,1,0:T(8,128)(2,1)S(1)} %collective-permute-done.3.refs_2_), channel_id=1, source_target_pairs={{0,8},{1,249},{2,10},{3,251},{4,12},{5,253},{6,14},{7,255},{8,16},... | collective-permute-start | bytes 786440 | tf_op jit(solution)/shard_map/ppermute | solution.py:418
  103.7 9.6 %collective-permute-start.18 = (bf16[66,16,128]{2,1,0:T(8,128)(2,1)S(1)}, bf16[66,16,128]{2,1,0:T(8,128)(2,1)S(1)}, u32[]{:S(2)}, u32[]{:S(2)}) collective-permute-start(bf16[66,16,128]{2,1,0:T(8,128)(2,1)S(1)} %get-tuple-element.83), channel_id=1, source_target_pairs={{0,8},{1,249},{2,10},{3,251},{4,12},{5,253},{6,14},{7,255},{8,16},... | collective-permute-start | bytes 811016 | tf_op jit(solution)/shard_map/ppermute | solution.py:418
  106.4 9.6 %collective-permute-start.5 = (bf16[64,16,128]{2,1,0:T(8,128)(2,1)S(1)}, bf16[64,16,128]{2,1,0:T(8,128)(2,1)S(1)}, u32[]{:S(2)}, u32[]{:S(2)}) collective-permute-start(bf16[64,16,128]{2,1,0:T(8,128)(2,1)S(1)} %collective-permute-done.4.refs_2_), channel_id=1, source_target_pairs={{0,8},{1,249},{2,10},{3,251},{4,12},{5,253},{6,14},{7,255},{8,16},... | collective-permute-start | bytes 786440 | tf_op jit(solution)/shard_map/ppermute | solution.py:418
  113.3 9.6 %collective-permute-start.19 = (bf16[66,16,128]{2,1,0:T(8,128)(2,1)S(1)}, bf16[66,16,128]{2,1,0:T(8,128)(2,1)S(1)}, u32[]{:S(2)}, u32[]{:S(2)}) collective-permute-start(bf16[66,16,128]{2,1,0:T(8,128)(2,1)S(1)} %get-tuple-element.87), channel_id=1, source_target_pairs={{0,8},{1,249},{2,10},{3,251},{4,12},{5,253},{6,14},{7,255},{8,16},... | collective-permute-start | bytes 811016 | tf_op jit(solution)/shard_map/ppermute | solution.py:418
  116.1 9.6 %collective-permute-start.6 = (bf16[64,16,128]{2,1,0:T(8,128)(2,1)S(1)}, bf16[64,16,128]{2,1,0:T(8,128)(2,1)S(1)}, u32[]{:S(2)}, u32[]{:S(2)}) collective-permute-start(bf16[64,16,128]{2,1,0:T(8,128)(2,1)S(1)} %collective-permute-done.5.refs_3_), channel_id=1, source_target_pairs={{0,8},{1,249},{2,10},{3,251},{4,12},{5,253},{6,14},{7,255},{8,16},... | collective-permute-start | bytes 786440 | tf_op jit(solution)/shard_map/ppermute | solution.py:418
  125.7 9.6 %collective-permute-start.7 = (bf16[64,16,128]{2,1,0:T(8,128)(2,1)S(1)}, bf16[64,16,128]{2,1,0:T(8,128)(2,1)S(1)}, u32[]{:S(2)}, u32[]{:S(2)}) collective-permute-start(bf16[64,16,128]{2,1,0:T(8,128)(2,1)S(1)} %collective-permute-done.6.refs_3_), channel_id=1, source_target_pairs={{0,8},{1,249},{2,10},{3,251},{4,12},{5,253},{6,14},{7,255},{8,16},... | collective-permute-start | bytes 786440 | tf_op jit(solution)/shard_map/ppermute | solution.py:418
  135.3 9.6 %collective-permute-start.8 = (bf16[64,16,128]{2,1,0:T(8,128)(2,1)S(1)}, bf16[64,16,128]{2,1,0:T(8,128)(2,1)S(1)}, u32[]{:S(2)}, u32[]{:S(2)}) collective-permute-start(bf16[64,16,128]{2,1,0:T(8,128)(2,1)S(1)} %collective-permute-done.7.refs_1_), channel_id=1, source_target_pairs={{0,8},{1,249},{2,10},{3,251},{4,12},{5,253},{6,14},{7,255},{8,16},... | collective-permute-start | bytes 786440 | tf_op jit(solution)/shard_map/ppermute | solution.py:418
  145.0 9.6 %collective-permute-start.9 = (bf16[64,16,128]{2,1,0:T(8,128)(2,1)S(1)}, bf16[64,16,128]{2,1,0:T(8,128)(2,1)S(1)}, u32[]{:S(2)}, u32[]{:S(2)}) collective-permute-start(bf16[64,16,128]{2,1,0:T(8,128)(2,1)S(1)} %collective-permute-done.8.refs_1_), channel_id=1, source_target_pairs={{0,8},{1,249},{2,10},{3,251},{4,12},{5,253},{6,14},{7,255},{8,16},... | collective-permute-start | bytes 786440 | tf_op jit(solution)/shard_map/ppermute | solution.py:418
  154.6 9.6 %collective-permute-start.10 = (bf16[64,16,128]{2,1,0:T(8,128)(2,1)S(1)}, bf16[64,16,128]{2,1,0:T(8,128)(2,1)S(1)}, u32[]{:S(2)}, u32[]{:S(2)}) collective-permute-start(bf16[64,16,128]{2,1,0:T(8,128)(2,1)S(1)} %collective-permute-done.9.refs_1_), channel_id=1, source_target_pairs={{0,8},{1,249},{2,10},{3,251},{4,12},{5,253},{6,14},{7,255},{8,16},... | collective-permute-start | bytes 786440 | tf_op jit(solution)/shard_map/ppermute | solution.py:418
  161.5 12.4 %collective-permute-start.24 = (bf16[66,16,128]{2,1,0:T(8,128)(2,1)S(1)}, bf16[66,16,128]{2,1,0:T(8,128)(2,1)S(1)}, u32[]{:S(2)}, u32[]{:S(2)}) collective-permute-start(bf16[66,16,128]{2,1,0:T(8,128)(2,1)S(1)} %get-tuple-element.107), channel_id=1, source_target_pairs={{0,8},{1,249},{2,10},{3,251},{4,12},{5,253},{6,14},{7,255},{8,16},... | collective-permute-start | bytes 811016 | tf_op jit(solution)/shard_map/ppermute | solution.py:418
  164.2 9.6 %collective-permute-start.11 = (bf16[64,16,128]{2,1,0:T(8,128)(2,1)S(1)}, bf16[64,16,128]{2,1,0:T(8,128)(2,1)S(1)}, u32[]{:S(2)}, u32[]{:S(2)}) collective-permute-start(bf16[64,16,128]{2,1,0:T(8,128)(2,1)S(1)} %collective-permute-done.10.block_a), channel_id=1, source_target_pairs={{0,8},{1,249},{2,10},{3,251},{4,12},{5,253},{6,14},{7,255},{8,16},... | collective-permute-start | bytes 786440 | tf_op jit(solution)/shard_map/ppermute | solution.py:418
  175.1 46.4 %all-to-all-start.1 = ((bf16[8,50,16,128]{3,2,1,0:T(8,128)(2,1)}), bf16[8,50,16,128]{3,2,1,0:T(8,128)(2,1)S(1)}, u32[]{:S(2)}, u32[]{:S(2)}) async-start(bf16[8,50,16,128]{3,2,1,0:T(8,128)(2,1)} %shard_map.139), calls=%async_computation.1 | async-start | bytes 3276800 | tf_op jit(solution)/shard_map/all_to_all | solution.py:568
  185.3 9.7 %collective-permute-start.25 = (bf16[56,16,128]{2,1,0:T(8,128)(2,1)S(1)}, bf16[56,16,128]{2,1,0:T(8,128)(2,1)S(1)}, u32[]{:S(2)}, u32[]{:S(2)}) collective-permute-start(bf16[56,16,128]{2,1,0:T(8,128)(2,1)S(1)} %get-tuple-element.109), channel_id=1, source_target_pairs={{0,8},{1,249},{2,10},{3,251},{4,12},{5,253},{6,14},{7,255},{8,16},... | collective-permute-start | bytes 688136 | tf_op jit(solution)/shard_map/ppermute | solution.py:418
  209.1 11.0 %collective-permute-start.32 = (bf16[10,16,128]{2,1,0:T(8,128)(2,1)S(1)}, bf16[10,16,128]{2,1,0:T(8,128)(2,1)S(1)}, u32[]{:S(2)}, u32[]{:S(2)}) collective-permute-start(bf16[10,16,128]{2,1,0:T(8,128)(2,1)S(1)} %get-tuple-element.116), channel_id=1, source_target_pairs={{0,8},{1,249},{2,10},{3,251},{4,12},{5,253},{6,14},{7,255},{8,16},... | collective-permute-start | bytes 122888 | tf_op jit(solution)/shard_map/ppermute | solution.py:418
  221.5 15.4 %all-to-all-start = ((bf16[8,18,16,128]{3,2,1,0:T(8,128)(2,1)}), bf16[8,18,16,128]{3,2,1,0:T(8,128)(2,1)S(1)}, u32[]{:S(2)}, u32[]{:S(2)}) async-start(bf16[8,18,16,128]{3,2,1,0:T(8,128)(2,1)} %shard_map.137), calls=%async_computation | async-start | bytes 1179648 | tf_op jit(solution)/shard_map/all_to_all | solution.py:586
  (32 other events, 328.1 us)
